TPU v7x, 32 devices: a whole 2x2x4 slice. The times are simulated.
32 devices in a mesh: gx: 4 (over y, x), gy: 8 (over z, core).
Axes of the slice: x: 2, y: 2, z: 4, core: 2. Of those that a mesh axis runs over, the one named last changes fastest.
Arguments:
- density: float32 [32, 32, 128], P('gx', 'gy'), may hold values from -5 to 5
- susceptibility: float32 [32, 32, 128], P('gx', 'gy'), may hold values from -5 to 5
- station_cell: int32 [2, 1024], P(None, 'gx'), may hold values from 0 to 1023
- station_line: int32 [2, 1024], P(None, 'gx'), may hold values from 0 to 255, as said below
- observed: float32 [2, 1024], P(None, 'gx'), may hold values from -3 to 3
- data_weight: float32 [2, 1024], P(None, 'gx'), may hold values from 0.5 to 2
- trial_steps: float32 [8], replicated, may hold values from 0.05 to 0.5
Outputs:
- data_gradient: float32 [2, 32, 32, 128], P(None, 'gx', 'gy')
- cross_force: float32 [2, 32, 32, 128], P(None, 'gx', 'gy')
- weighted_residual: float32 [2, 1024], P(None, 'gx')
- trial_values: float32 [8], replicated
Inputs may be any that keep to these rules, and one draw needn't show every extreme that they name: `station_line`: one or more survey lines hold no station of either field.
All inputs are finite; a program needn't handle non-finite values. Where the computation divides by a largest or mean magnitude, that divisor is 1e-20 or more.
Results may differ from a plain program's by a relative error of at most 0.0003.
Values sent between devices are 32-bit elements; how exact they have to be, the bound alone decides.
A program may use at most 64 MiB of HBM per device.

v0:
```python
import math

import jax
import jax.numpy as jnp
from jax import lax
from jax.sharding import PartitionSpec as P

LINES = 256


cell_depth = 2.0
lift = 1.0
coupling_scale = 0.05
highest = lax.Precision.HIGHEST


def extended_2(block, sides, width):
    for axis, dim in sides:
        count = lax.axis_size(axis)
        forward = [(i, i + 1) for i in range(count - 1)]
        backward = [(target, source) for source, target in forward]
        low = lax.ppermute(
            lax.slice_in_dim(block, block.shape[dim] - width, None, axis=dim), axis, forward
        )
        high = lax.ppermute(lax.slice_in_dim(block, 0, width, axis=dim), axis, backward)
        block = jnp.concatenate([low, block, high], axis=dim)
    return block


def kernel_tile(field, station_x, station_y, cell_x, cell_y, depth):
    gap_x = station_x[:, None] - cell_x[None, :]
    gap_y = station_y[:, None] - cell_y[None, :]
    depth_row = depth[None, :]
    radius_sq = gap_x * gap_x + gap_y * gap_y + depth_row * depth_row
    inverse = lax.rsqrt(radius_sq)
    cube = inverse * inverse * inverse
    if field == 0:
        return depth_row * cube
    return (3.0 * depth_row * depth_row - radius_sq) * cube * inverse * inverse


def cell_coords(anchor_x, anchor_y, width, layers, start, count):
    position = start + jnp.arange(count, dtype=jnp.int32)
    cell_x = (anchor_x + position // (width * layers)).astype(jnp.float32)
    cell_y = (anchor_y + position // layers % width).astype(jnp.float32)
    depth = ((position % layers).astype(jnp.float32) + 0.5) * cell_depth + lift
    return (cell_x, cell_y, depth)


def to_blocks(values, size):
    return jnp.swapaxes(values.reshape(2, -1, size), 0, 1)


def forward_part(models, anchor_x, anchor_y, station_x, station_y):
    rows, width, layers = (models.shape[1], models.shape[2], models.shape[3])
    cells = rows * width * layers
    flat = models.reshape(2, cells)
    cell_block = math.gcd(cells, 2048)
    station_block = math.gcd(station_x.shape[1], 64)

    def forward_station_turn(pair):
        block_x, block_y = pair

        def forward_cell_turn(index, total):
            start = index * cell_block
            cell_x, cell_y, depth = cell_coords(
                anchor_x, anchor_y, width, layers, start, cell_block
            )
            piece = lax.dynamic_slice_in_dim(flat, start, cell_block, 1)
            rows_out = [
                jnp.dot(
                    kernel_tile(field, block_x[field], block_y[field], cell_x, cell_y, depth),
                    piece[field],
                    precision=highest,
                )
                for field in range(2)
            ]
            return total + jnp.stack(rows_out)

        return lax.fori_loop(
            0, cells // cell_block, forward_cell_turn, jnp.zeros((2, station_block), jnp.float32)
        )

    parts = lax.map(
        forward_station_turn,
        (to_blocks(station_x, station_block), to_blocks(station_y, station_block)),
    )
    return jnp.swapaxes(parts, 0, 1).reshape(2, -1)


def adjoint_part(source, anchor_x, anchor_y, rows, width, layers, station_x, station_y):
    cells = rows * width * layers
    cell_block = math.gcd(cells, 2048)
    station_block = math.gcd(station_x.shape[1], 64)

    def adjoint_cell_turn(index):
        start = index * cell_block
        cell_x, cell_y, depth = cell_coords(anchor_x, anchor_y, width, layers, start, cell_block)

        def cell_station_turn(turn, total):
            first = turn * station_block
            block_x = lax.dynamic_slice_in_dim(station_x, first, station_block, 1)
            block_y = lax.dynamic_slice_in_dim(station_y, first, station_block, 1)
            block_source = lax.dynamic_slice_in_dim(source, first, station_block, 1)
            rows_out = [
                jnp.dot(
                    block_source[field],
                    kernel_tile(field, block_x[field], block_y[field], cell_x, cell_y, depth),
                    precision=highest,
                )
                for field in range(2)
            ]
            return total + jnp.stack(rows_out)

        return lax.fori_loop(
            0,
            station_x.shape[1] // station_block,
            cell_station_turn,
            jnp.zeros((2, cell_block), jnp.float32),
        )

    parts = lax.map(adjoint_cell_turn, jnp.arange(cells // cell_block, dtype=jnp.int32))
    return jnp.swapaxes(parts, 0, 1).reshape(2, rows, width, layers)


def cross_terms(extended, start_x, start_y, total_x, total_y):
    rows = extended.shape[1] - 1
    width = extended.shape[2] - 1
    global_x = start_x - 1 + jnp.arange(rows, dtype=jnp.int32)
    global_y = start_y - 1 + jnp.arange(width, dtype=jnp.int32)
    mask_x = (global_x < total_x - 1).astype(jnp.float32)[:, None, None]
    mask_y = (global_y < total_y - 1).astype(jnp.float32)[None, :, None]
    valid = ((global_x >= 0)[:, None] & (global_y >= 0)[None, :]).astype(jnp.float32)[:, :, None]

    def diffs(field):
        base = field[:-1, :-1, :]
        along_x = (field[1:, :-1, :] - base) * mask_x
        along_y = (field[:-1, 1:, :] - base) * mask_y
        along_z = jnp.concatenate(
            [base[:, :, 1:] - base[:, :, :-1], jnp.zeros_like(base[:, :, :1])], axis=2
        )
        return (along_x, along_y, along_z)

    first_x, first_y, first_z = diffs(extended[0])
    second_x, second_y, second_z = diffs(extended[1])
    part_one = first_y * second_z - first_z * second_y
    part_two = first_z * second_x - first_x * second_z
    part_three = first_x * second_y - first_y * second_x
    return (part_one * part_one + part_two * part_two + part_three * part_three) * valid


def line_totals(values, lines):
    labels = jnp.arange(LINES, dtype=jnp.int32)
    onehot = (lines[:, :, None] == labels).astype(jnp.float32)
    local = jnp.einsum("fs,fsl->fl", values, onehot, precision=highest)
    return lax.psum(local, "gx")


def spread_table(table, lines):
    labels = jnp.arange(LINES, dtype=jnp.int32)
    onehot = (lines[:, :, None] == labels).astype(jnp.float32)
    return jnp.einsum("fl,fsl->fs", table, onehot, precision=highest)


def faces(fields):
    return extended_2(fields, (("gx", 1), ("gy", 2)), 1)


def body(density, susceptibility, station_cell, station_line, observed, data_weight, trial_steps):
    rows, width, layers = density.shape
    groups = lax.axis_size("gx")
    columns = lax.axis_size("gy")
    total_x = rows * groups
    total_y = width * columns
    own_count = station_cell.shape[1]
    total_stations = own_count * groups
    anchor_x = lax.axis_index("gx") * rows
    anchor_y = lax.axis_index("gy") * width
    models = jnp.stack([density, susceptibility])
    own_x = (station_cell // total_y).astype(jnp.float32)
    own_y = (station_cell % total_y).astype(jnp.float32)
    coupling = coupling_scale * total_stations / (total_x * total_y * layers)

    def energies(extended):
        squares = cross_terms(extended, anchor_x, anchor_y, total_x, total_y)
        return (0.5 * jnp.sum(squares), 0.5 * jnp.sum(squares[1:, 1:]))

    extended = faces(models)
    (rim_energy, model_energy), rim_grad = jax.value_and_grad(energies, has_aux=True)(extended)
    cross_force = rim_grad[:, 1:-1, 1:-1, :]

    def fold_forward(piece, start):
        return forward_part(piece, start, anchor_y, own_x, own_y)

    def column_data(fields):
        partial_value = fold_forward(lax.all_gather(fields, "gx", axis=1, tiled=True), jnp.int32(0))
        return lax.psum(partial_value, "gy")

    predicted = column_data(models)
    misfit = predicted - observed
    both_lines = jnp.concatenate([station_line, station_line])
    first_totals = line_totals(jnp.concatenate([misfit, jnp.ones_like(misfit)]), both_lines)
    counts = jnp.maximum(first_totals[2:], 1.0)
    residual = misfit - spread_table(first_totals[:2] / counts, station_line)
    weighted_residual = data_weight * residual
    source = data_weight * weighted_residual
    source = source - spread_table(line_totals(source, station_line) / counts, station_line)
    data_gradient = jnp.swapaxes(
        lax.psum_scatter(
            jnp.swapaxes(
                adjoint_part(
                    source,
                    jnp.int32(0),
                    anchor_y,
                    lax.axis_size("gx") * rows,
                    width,
                    layers,
                    own_x,
                    own_y,
                ),
                0,
                1,
            ),
            "gx",
            scatter_dimension=0,
            tiled=True,
        ),
        0,
        1,
    )
    gradient = data_gradient + coupling * cross_force
    peak = lax.pmax(jnp.max(jnp.abs(gradient)), ("gx", "gy")) + 1e-06
    direction = gradient / peak
    extended_direction = faces(direction)
    image = column_data(direction)
    change = image - spread_table(line_totals(image, station_line) / counts, station_line)
    shares = []
    for trial in range(trial_steps.shape[0]):
        step = trial_steps[trial]
        moved = data_weight * (residual - step * change)
        data_value = 0.5 * jnp.sum(moved * moved)
        own_extended = extended - step * extended_direction
        shares.append(
            data_value / columns
            + coupling
            * (
                0.5
                * jnp.sum(cross_terms(own_extended, anchor_x, anchor_y, total_x, total_y)[1:, 1:])
            )
        )
    trial_values = lax.psum(jnp.stack(shares), ("gx", "gy")) / (2 * total_stations)
    return (data_gradient, cross_force, weighted_residual, trial_values)


def solution(mesh):
    placed = (
        P("gx", "gy", None),
        P("gx", "gy", None),
        P(None, "gx"),
        P(None, "gx"),
        P(None, "gx"),
        P(None, "gx"),
        P(),
    )
    return jax.shard_map(
        body,
        mesh=mesh,
        in_specs=placed,
        out_specs=(P(None, "gx", "gy", None), P(None, "gx", "gy", None), P(None, "gx"), P()),
        check_vma=False,
    )
```

profile of v0, /device:TPU:0, one launch (start us, length us, event | category | flops | bytes accessed | tf_op | source)
XLA Modules:
  0.0 424.1 jit_solution(3316433478356458403)
XLA Ops:
  14.2 10.6 %all_gather.6 = f32[2,32,4,128]{3,2,1,0:T(4,128)S(1)} all-gather(f32[2,8,4,128]{3,2,1,0:T(4,128)S(1)} %pad_maximum_fusion.2), channel_id=1, replica_groups=mesh['gx'=4,'gy'=8] {'gx'}, dimensions={1}, use_global_device_ids=true | all-gather | bytes 163840 | tf_op jit(solution)/shard_map/all_gather | solution.py:196
  25.7 53.3 %while.116 = (s32[]{:T(128)}, f32[4,2,64]{2,1,0:T(2,128)S(1)}, f32[4,2,64]{2,1,0:T(2,128)S(1)}, f32[4,2,64]{2,1,0:T(2,128)S(1)}, s32[]{:T(128)}, /*index=5*/f32[...) while((s32[]{:T(128)}, f32[4,2,64]{2,1,0:T(2,128)S(1)}, ...), condition=%wide.region_3.4_spmd, body=%wide.region_0.3_spmd.sunk | while | flops 6052234 | bytes 133554 | solution.py:84
  25.7 13.3 %while.121 = (s32[]{:T(128)}, f32[2,64]{1,0:T(2,128)S(1)}, f32[2,64]{1,0:T(2,128)S(1)}, f32[2,64]{1,0:T(2,128)S(1)}, s32[]{:T(128)}, /*index=5*/f32[2,16384]{1,0...) while((s32[]{:T(128)}, f32[2,64]{1,0:T(2,128)S(1)}, ...), condition=%wide.region_2.2_spmd.clone, body=%wide.region_1.1_spmd.clone.sunk | while | flops 6052232 | bytes 129229 | solution.py:80
  39.0 13.3 %while.121 = (s32[]{:T(128)}, f32[2,64]{1,0:T(2,128)S(1)}, f32[2,64]{1,0:T(2,128)S(1)}, f32[2,64]{1,0:T(2,128)S(1)}, s32[]{:T(128)}, /*index=5*/f32[2,16384]{1,0...) while((s32[]{:T(128)}, f32[2,64]{1,0:T(2,128)S(1)}, ...), condition=%wide.region_2.2_spmd.clone, body=%wide.region_1.1_spmd.clone.sunk | while | flops 6052232 | bytes 129229 | solution.py:80
  52.4 13.3 %while.121 = (s32[]{:T(128)}, f32[2,64]{1,0:T(2,128)S(1)}, f32[2,64]{1,0:T(2,128)S(1)}, f32[2,64]{1,0:T(2,128)S(1)}, s32[]{:T(128)}, /*index=5*/f32[2,16384]{1,0...) while((s32[]{:T(128)}, f32[2,64]{1,0:T(2,128)S(1)}, ...), condition=%wide.region_2.2_spmd.clone, body=%wide.region_1.1_spmd.clone.sunk | while | flops 6052232 | bytes 129229 | solution.py:80
  65.7 13.3 %while.121 = (s32[]{:T(128)}, f32[2,64]{1,0:T(2,128)S(1)}, f32[2,64]{1,0:T(2,128)S(1)}, f32[2,64]{1,0:T(2,128)S(1)}, s32[]{:T(128)}, /*index=5*/f32[2,16384]{1,0...) while((s32[]{:T(128)}, f32[2,64]{1,0:T(2,128)S(1)}, ...), condition=%wide.region_2.2_spmd.clone, body=%wide.region_1.1_spmd.clone.sunk | while | flops 6052232 | bytes 129229 | solution.py:80
  79.1 14.1 %psum.42 = f32[2,256]{1,0:T(2,128)S(1)} all-reduce(f32[2,256]{1,0:T(2,128)S(1)} %reshape.283), channel_id=1, replica_groups=mesh['gx'=4,'gy'=8] {'gy'}, use_global_device_ids=true, to_apply=%region_4.5 | all-reduce | flops 512 | bytes 4096 | tf_op jit(solution)/shard_map/psum | solution.py:197
  94.4 8.9 %psum.43 = f32[4,256]{1,0:T(4,128)S(1)} all-reduce(f32[4,256]{1,0:T(4,128)S(1)} %bitcast.234), channel_id=1, replica_groups=mesh['gx'=4,'gy'=8] {'gx'}, use_global_device_ids=true, to_apply=%region_5.6 | all-reduce | flops 1024 | bytes 8192 | tf_op jit(solution)/shard_map/psum | solution.py:156
  104.9 8.3 %psum.44 = f32[2,256]{1,0:T(2,128)S(1)} all-reduce(f32[2,256]{1,0:T(2,128)S(1)} %bitcast.238), channel_id=1, replica_groups=mesh['gx'=4,'gy'=8] {'gx'}, use_global_device_ids=true, to_apply=%region_6.7 | all-reduce | flops 512 | bytes 4096 | tf_op jit(solution)/shard_map/psum | solution.py:156
  113.6 60.8 %while.118 = (s32[]{:T(128)}, f32[8,2,2048]{2,1,0:T(2,128)S(1)}, s32[8]{0:T(128)S(1)}, s32[]{:T(128)}, f32[2,256]{1,0:T(2,128)S(1)}, /*index=5*/f32[2,256]{1,0:T...) while((s32[]{:T(128)}, f32[8,2,2048]{2,1,0:T(2,128)S(1)}, ...), condition=%wide.region_10.11_spmd, body=%wide.region_7.10_spmd.sunk | while | flops 6064138 | bytes 213438 | solution.py:122
  114.9 6.3 %while.122 = (s32[]{:T(128)}, f32[2,2048]{1,0:T(2,128)S(1)}, f32[2,256]{1,0:T(2,128)S(1)}, f32[2,256]{1,0:T(2,128)S(1)}, f32[2,256]{1,0:T(2,128)S(1)}, /*index=5...) while((s32[]{:T(128)}, f32[2,2048]{1,0:T(2,128)S(1)}, ...), condition=%wide.region_9.9_spmd.clone.clone.clone, body=%wide.region_8.8_spmd.clone.clone.clone.sunk | while | flops 6064135 | bytes 180413 | solution.py:115
  122.5 6.3 %while.122 = (s32[]{:T(128)}, f32[2,2048]{1,0:T(2,128)S(1)}, f32[2,256]{1,0:T(2,128)S(1)}, f32[2,256]{1,0:T(2,128)S(1)}, f32[2,256]{1,0:T(2,128)S(1)}, /*index=5...) while((s32[]{:T(128)}, f32[2,2048]{1,0:T(2,128)S(1)}, ...), condition=%wide.region_9.9_spmd.clone.clone.clone, body=%wide.region_8.8_spmd.clone.clone.clone.sunk | while | flops 6064135 | bytes 180413 | solution.py:115
  137.7 6.3 %while.122 = (s32[]{:T(128)}, f32[2,2048]{1,0:T(2,128)S(1)}, f32[2,256]{1,0:T(2,128)S(1)}, f32[2,256]{1,0:T(2,128)S(1)}, f32[2,256]{1,0:T(2,128)S(1)}, /*index=5...) while((s32[]{:T(128)}, f32[2,2048]{1,0:T(2,128)S(1)}, ...), condition=%wide.region_9.9_spmd.clone.clone.clone, body=%wide.region_8.8_spmd.clone.clone.clone.sunk | while | flops 6064135 | bytes 180413 | solution.py:115
  181.4 33.5 %all-reduce.34.cloned.1.call-done = f32[32,2,4,128]{3,2,0,1:T(4,128)} async-done(((f32[32,2,4,128]{3,2,0,1:T(4,128)}), f32[32,2,4,128]{3,2,0,1:T(4,128)}) %all-reduce.34.cloned.1.call-update) | async-done | bytes 131088
  216.3 39.4 %pmax.7 = f32[]{:T(128)} all-reduce(f32[]{:T(128)} %get-tuple-element.1187), channel_id=1, replica_groups=mesh['gx'=4,'gy'=8] {'gx','gy'}, use_global_device_ids=true, to_apply=%region_13.14 | all-reduce | flops 1 | bytes 8 | tf_op jit(solution)/shard_map/pmax | solution.py:232
  256.5 9.5 %all_gather.7 = f32[2,32,4,128]{3,2,1,0:T(4,128)S(1)} all-gather(f32[2,8,4,128]{3,2,1,0:T(4,128)S(1)} %broadcast_divide_fusion), channel_id=1, replica_groups=mesh['gx'=4,'gy'=8] {'gx'}, dimensions={1}, use_global_device_ids=true | all-gather | bytes 163840 | tf_op jit(solution)/shard_map/all_gather | solution.py:196
  270.7 53.4 %while.120 = (s32[]{:T(128)}, f32[4,2,64]{2,1,0:T(2,128)S(1)}, f32[4,2,64]{2,1,0:T(2,128)S(1)}, f32[4,2,64]{2,1,0:T(2,128)S(1)}, s32[]{:T(128)}, /*index=5*/f32[...) while((s32[]{:T(128)}, f32[4,2,64]{2,1,0:T(2,128)S(1)}, ...), condition=%wide.region_17.18_spmd, body=%wide.region_14.17_spmd.sunk | while | flops 6052234 | bytes 133554 | solution.py:84
  270.8 13.3 %while.123 = (s32[]{:T(128)}, f32[2,64]{1,0:T(2,128)S(1)}, f32[2,64]{1,0:T(2,128)S(1)}, f32[2,64]{1,0:T(2,128)S(1)}, s32[]{:T(128)}, /*index=5*/f32[2,16384]{1,0...) while((s32[]{:T(128)}, f32[2,64]{1,0:T(2,128)S(1)}, ...), condition=%wide.region_16.16_spmd.clone, body=%wide.region_15.15_spmd.clone.sunk | while | flops 6052232 | bytes 129229 | solution.py:80
  284.1 13.3 %while.123 = (s32[]{:T(128)}, f32[2,64]{1,0:T(2,128)S(1)}, f32[2,64]{1,0:T(2,128)S(1)}, f32[2,64]{1,0:T(2,128)S(1)}, s32[]{:T(128)}, /*index=5*/f32[2,16384]{1,0...) while((s32[]{:T(128)}, f32[2,64]{1,0:T(2,128)S(1)}, ...), condition=%wide.region_16.16_spmd.clone, body=%wide.region_15.15_spmd.clone.sunk | while | flops 6052232 | bytes 129229 | solution.py:80
  297.5 13.3 %while.123 = (s32[]{:T(128)}, f32[2,64]{1,0:T(2,128)S(1)}, f32[2,64]{1,0:T(2,128)S(1)}, f32[2,64]{1,0:T(2,128)S(1)}, s32[]{:T(128)}, /*index=5*/f32[2,16384]{1,0...) while((s32[]{:T(128)}, f32[2,64]{1,0:T(2,128)S(1)}, ...), condition=%wide.region_16.16_spmd.clone, body=%wide.region_15.15_spmd.clone.sunk | while | flops 6052232 | bytes 129229 | solution.py:80
  310.8 13.3 %while.123 = (s32[]{:T(128)}, f32[2,64]{1,0:T(2,128)S(1)}, f32[2,64]{1,0:T(2,128)S(1)}, f32[2,64]{1,0:T(2,128)S(1)}, s32[]{:T(128)}, /*index=5*/f32[2,16384]{1,0...) while((s32[]{:T(128)}, f32[2,64]{1,0:T(2,128)S(1)}, ...), condition=%wide.region_16.16_spmd.clone, body=%wide.region_15.15_spmd.clone.sunk | while | flops 6052232 | bytes 129229 | solution.py:80
  324.2 13.6 %psum.45 = f32[2,256]{1,0:T(2,128)S(1)} all-reduce(f32[2,256]{1,0:T(2,128)S(1)} %reshape.286), channel_id=1, replica_groups=mesh['gx'=4,'gy'=8] {'gy'}, use_global_device_ids=true, to_apply=%region_18.19 | all-reduce | flops 512 | bytes 4096 | tf_op jit(solution)/shard_map/psum | solution.py:197
  338.1 10.1 %psum.46 = f32[2,256]{1,0:T(2,128)S(1)} all-reduce(f32[2,256]{1,0:T(2,128)S(1)} %bitcast.239), channel_id=1, replica_groups=mesh['gx'=4,'gy'=8] {'gx'}, use_global_device_ids=true, to_apply=%region_19.20 | all-reduce | flops 512 | bytes 4096 | tf_op jit(solution)/shard_map/psum | solution.py:156
  376.7 40.0 %psum.47 = f32[8]{0:T(128)S(1)} all-reduce(f32[8]{0:T(128)S(1)} %stack.131), channel_id=1, replica_groups=mesh['gx'=4,'gy'=8] {'gx','gy'}, use_global_device_ids=true, to_apply=%region_36.37 | all-reduce | flops 8 | bytes 64 | tf_op jit(solution)/shard_map/psum | solution.py:251
  (959 shorter events, 231.9 us)
Async XLA Ops:
  7.2 207.8 %all-reduce.34.cloned.1.call-start = ((), (), s32[]{:S(2)}) async-start(), calls=%async_computation | async-start | bytes 262144
  7.2 6.9 %copy-start = (f32[8,4,128]{2,1,0:T(4,128)S(1)}, f32[8,4,128]{2,1,0:T(4,128)}, u32[]{:S(2)}) copy-start(f32[8,4,128]{2,1,0:T(4,128)} %param.19) | copy-start | bytes 49156
  7.2 6.9 %copy-start.1 = (f32[8,4,128]{2,1,0:T(4,128)S(1)}, f32[8,4,128]{2,1,0:T(4,128)}, u32[]{:S(2)}) copy-start(f32[8,4,128]{2,1,0:T(4,128)} %param.20) | copy-start | bytes 49156
  8.0 167.5 %collective-permute-start = (f32[2,1,4,128]{3,2,1,0:T(4,128)S(1)}, f32[2,1,4,128]{3,2,1,0:T(4,128)S(1)}, u32[]{:S(2)}, u32[]{:S(2)}) collective-permute-start(f32[2,1,4,128]{3,2,1,0:T(4,128)S(1)} %get-tuple-element.1306), channel_id=1, source_target_pairs={{0,8},{8,16},{16,24},{1,9},{9,17},{17,25},{2,10},{10,18},{18,26},{... | collective-permute-start | bytes 12296 | tf_op jit(solution)/shard_map/ppermute | solution.py:22
  12.9 162.7 %collective-permute-start.1 = (f32[2,1,4,128]{3,2,1,0:T(4,128)S(1)}, f32[2,1,4,128]{3,2,1,0:T(4,128)S(1)}, u32[]{:S(2)}, u32[]{:S(2)}) collective-permute-start(f32[2,1,4,128]{3,2,1,0:T(4,128)S(1)} %get-tuple-element.1307), channel_id=1, source_target_pairs={{8,0},{16,8},{24,16},{9,1},{17,9},{25,17},{10,2},{18,10},{26,18},{... | collective-permute-start | bytes 12296 | tf_op jit(solution)/shard_map/ppermute | solution.py:25
  24.8 0.7 copy-start.6
  79.1 14.1 %copy-start.7 = (f32[2,256]{1,0:T(2,128)S(1)}, f32[2,256]{1,0:T(2,128)}, u32[]{:S(2)}) copy-start(f32[2,256]{1,0:T(2,128)} %param.23) | copy-start | bytes 6148
  93.2 0.7 copy-start.8
  103.3 0.7 copy-start.5
  175.6 2.6 copy-start.4
  175.6 5.3 %collective-permute-start.2 = (f32[2,10,1,128]{3,2,1,0:T(1,128)S(1)}, f32[2,10,1,128]{3,2,1,0:T(1,128)S(1)}, u32[]{:S(2)}, u32[]{:S(2)}) collective-permute-start(f32[2,10,1,128]{3,2,1,0:T(1,128)S(1)} %get-tuple-element.1302), channel_id=1, source_target_pairs={{0,1},{1,2},{2,3},{3,4},{4,5},{5,6},{6,7},{8,9},{9,10},{10,11},{11... | collective-permute-start | bytes 30728 | tf_op jit(solution)/shard_map/ppermute | solution.py:22
  176.9 4.0 collective-permute-start.3
  178.9 0.7 copy-start.9
  216.3 40.1 %copy-start.2 = (f32[2,8,4,128]{3,2,1,0:T(4,128)}, f32[2,8,4,128]{3,2,1,0:T(4,128)S(1)}, u32[]{:S(2)}) copy-start(f32[2,8,4,128]{3,2,1,0:T(4,128)S(1)} %get-tuple-element.1188) | copy-start | bytes 98308
  216.3 40.1 %copy-start.3 = (f32[2,8,4,128]{3,2,1,0:T(4,128)}, f32[2,8,4,128]{3,2,1,0:T(4,128)S(1)}, u32[]{:S(2)}) copy-start(f32[2,8,4,128]{3,2,1,0:T(4,128)S(1)} %get-tuple-element.1189) | copy-start | bytes 98308
  266.0 82.6 %collective-permute-start.4 = (f32[2,1,4,128]{3,2,1,0:T(4,128)S(1)}, f32[2,1,4,128]{3,2,1,0:T(4,128)S(1)}, u32[]{:S(2)}, u32[]{:S(2)}) collective-permute-start(f32[2,1,4,128]{3,2,1,0:T(4,128)S(1)} %get-tuple-element.1304), channel_id=1, source_target_pairs={{0,8},{8,16},{16,24},{1,9},{9,17},{17,25},{2,10},{10,18},{18,26},{... | collective-permute-start | bytes 12296 | tf_op jit(solution)/shard_map/ppermute | solution.py:22
  269.3 79.3 %collective-permute-start.5 = (f32[2,1,4,128]{3,2,1,0:T(4,128)S(1)}, f32[2,1,4,128]{3,2,1,0:T(4,128)S(1)}, u32[]{:S(2)}, u32[]{:S(2)}) collective-permute-start(f32[2,1,4,128]{3,2,1,0:T(4,128)S(1)} %get-tuple-element.1305), channel_id=1, source_target_pairs={{8,0},{16,8},{24,16},{9,1},{17,9},{25,17},{10,2},{18,10},{26,18},{... | collective-permute-start | bytes 12296 | tf_op jit(solution)/shard_map/ppermute | solution.py:25
  348.6 13.2 %collective-permute-start.6 = (f32[2,10,1,128]{3,2,1,0:T(1,128)S(1)}, f32[2,10,1,128]{3,2,1,0:T(1,128)S(1)}, u32[]{:S(2)}, u32[]{:S(2)}) collective-permute-start(f32[2,10,1,128]{3,2,1,0:T(1,128)S(1)} %get-tuple-element.1300), channel_id=1, source_target_pairs={{0,1},{1,2},{2,3},{3,4},{4,5},{5,6},{6,7},{8,9},{9,10},{10,11},{11... | collective-permute-start | bytes 30728 | tf_op jit(solution)/shard_map/ppermute | solution.py:22
  349.9 11.9 %collective-permute-start.7 = (f32[2,10,1,128]{3,2,1,0:T(1,128)S(1)}, f32[2,10,1,128]{3,2,1,0:T(1,128)S(1)}, u32[]{:S(2)}, u32[]{:S(2)}) collective-permute-start(f32[2,10,1,128]{3,2,1,0:T(1,128)S(1)} %get-tuple-element.1301), channel_id=1, source_target_pairs={{1,0},{2,1},{3,2},{4,3},{5,4},{6,5},{7,6},{9,8},{10,9},{11,10},{12... | collective-permute-start | bytes 30728 | tf_op jit(solution)/shard_map/ppermute | solution.py:25
Sparse Core Ops, SparseCore 0:
  175.5 39.4 all-reduce.33
where the time goes:
time: 426 us; the launch traced here: 424 us
  blocking collectives  155 us (36%)
  matrix products  140 us (33%)
  waiting for transfers between devices  33.6 us (8%)
  other arithmetic  28.7 us (7%)
  between operations  26 us (6%)
  starting transfers between devices  16 us (4%)
  local copies, waits for them, and re-layouts  15.6 us (4%)
  loops' own time  9.71 us (2%)
    dot_general x128, matrix products, forward_cell_turn(): jnp.dot(kernel_tile(field, block_x[field], block_y[field], cell_x, cell_y...  97.5 us
    dot_general x64, matrix products, cell_station_turn(): jnp.dot(block_source[field], kernel_tile(field, block_x[field], block_y[f...  40.2 us
    psum x1, blocking collectives, body(): lax.psum(jnp.stack(shares), ('gx', 'gy')) / (2 * total_stations)  40 us
    pmax x1, blocking collectives, body(): peak = lax.pmax(jnp.max(jnp.abs(gradient)), ('gx', 'gy')) + 1e-06  39.4 us
    unnamed x2, waiting for transfers between devices  33.6 us
    psum x2, blocking collectives, column_data(): return lax.psum(partial_value, 'gy')  27.7 us
    psum x3, blocking collectives, line_totals(): return lax.psum(local, 'gx')  27.3 us
    all_gather x2, blocking collectives, column_data(): lax.all_gather(fields, 'gx', axis=1, tiled=True)  20.1 us
  transfers between devices with their start and end apart: 9, of which 1 were waited for; matrix products, arithmetic and copies ran while one was open for 40% of the time, Pallas kernels for 0%

commit v1 on v0

v1 whole, which is shorter than its diff:
```python
import functools

import jax
import jax.numpy as jnp
from jax import lax
from jax.experimental import pallas as pl
from jax.experimental.pallas import tpu as pltpu
from jax.sharding import PartitionSpec as P

LINES = 256
LOW = 32
HIGH = LINES // LOW

cell_depth = 2.0
lift = 1.0
coupling_scale = 0.05

MESH = pl.DeviceIdType.MESH
f32 = jnp.float32
bf16 = jnp.bfloat16
NN = (((1,), (0,)), ((), ()))
NT = (((1,), (1,)), ((), ()))


def iota(shape, dim):
    return lax.broadcasted_iota(jnp.int32, shape, dim)


def split2(x):
    high = x.astype(bf16)
    return high, (x - high.astype(f32)).astype(bf16)


def split3(x):
    high = x.astype(bf16)
    rest = x - high.astype(f32)
    middle = rest.astype(bf16)
    return high, middle, (rest - middle.astype(f32)).astype(bf16)


def thirds(x):
    n = x.shape[0] // 3
    return x[:n] + x[n : 2 * n] + x[2 * n :]


def cross(a, b):
    return (a[1] * b[2] - a[2] * b[1], a[2] * b[0] - a[0] * b[2], a[0] * b[1] - a[1] * b[0])


def dot3(a, b):
    return a[0] * b[0] + a[1] * b[1] + a[2] * b[2]


def total(x):
    return jnp.sum(jnp.sum(x, axis=0, keepdims=True), axis=1, keepdims=True)


def largest(x):
    return jnp.max(jnp.max(x, axis=0, keepdims=True), axis=1, keepdims=True)


def kernel(
    G, C, den, sus, cell, line, obs, wgt, steps,
    dg_out, cf_out, wr_out, tv_out,
    E2, RS, F, A, cellb, lineb, obsb, wgtb, OY, OX, OHI, OLO, wrs,
    b1, b2, c1, c2, s1, s2, M, SH, RH, CH, CR, CFX, GE,
    s_st, r_st, s_h, r_h, s_c, r_c, s_b1, r_b1, s_b2, r_b2, s_c1, r_c1, s_c2, r_c2, s_s1, r_s1, s_s2, r_s2,
):
    R, W, K = den.shape
    own = cell.shape[1]
    NX, NY = R * G, W * C
    V = 2 * NY
    xp = 128 // V
    Q = NX // xp
    N = E2.shape[2]
    nch = N // 128
    ST = 2 * own * G
    T = steps.shape[0]
    mx = lax.axis_index("gx")
    my = lax.axis_index("gy")
    x0 = mx * R
    y0 = my * W
    total_stations = own * G
    coupling = coupling_scale * total_stations / (NX * NY * K)

    def at(dx, dy):
        return (lax.rem(mx + dx + G, G), lax.rem(my + dy + C, C))

    ycast = [at(0, d) for d in range(1, C)]
    xcast = [at(d, 0) for d in range(1, G)]
    diagonal = [at(1, -1), at(-1, 1)]
    barrier = pltpu.get_barrier_semaphore()
    partners = ycast + xcast + diagonal
    for where in partners:
        pl.semaphore_signal(barrier, inc=1, device_id=where, device_id_type=MESH)

    lane = iota((1, 128), 1)

    h_col = (iota((K, 128), 0).astype(f32) + 0.5) * cell_depth + lift
    h2 = h_col * h_col

    def table_turn(n, carry):
        gap_x = (n * xp + lane // V - 8 - x0).astype(f32)
        gap_y = (lane % V - 4 - y0).astype(f32)
        r2 = (gap_x * gap_x + gap_y * gap_y) + h2
        inverse = lax.rsqrt(r2)
        inverse2 = inverse * inverse
        cube = inverse2 * inverse
        both = (h_col * cube, (3.0 * h2 - r2) * cube * inverse2)
        spot = pl.ds(pl.multiple_of(n * 128, 128), 128)
        for f in range(2):
            high, low = split2(both[f])
            E2[f, 0:K, spot] = high
            E2[f, K : 2 * K, spot] = low
        return carry

    lax.fori_loop(0, nch, table_turn, 0)

    in_y = (lane % V) < NY

    def forward(columns, f):
        x = jnp.concatenate(columns, axis=0)
        high, low = split2(x)
        left = jnp.concatenate(
            [jnp.concatenate([high, high], axis=1), jnp.concatenate([low, low], axis=1)], axis=0
        )
        t = lax.dot_general(left, E2[f], NN, preferred_element_type=f32)
        t = t[: R * W] + t[R * W :]
        t2 = sum(pltpu.roll(t[j * R : (j + 1) * R], N - (4 - j), 1) for j in range(W))
        shifted = [t2] + [pltpu.roll(t2, N - c * V, 1) for c in range(1, xp)]
        sub = iota((R, NX * V), 0)
        acc = jnp.zeros((R, NX * V), f32)
        for i in range(R):
            s = 8 - i
            first = (s // xp) * 128
            acc = jnp.where(sub == i, shifted[s % xp][:, first : first + NX * V], acc)
        row = jnp.sum(acc, axis=0, keepdims=True)
        grid = jnp.concatenate([row[:, q * 128 : (q + 1) * 128] for q in range(Q)], axis=0)
        grid = jnp.where(in_y, grid, 0.0)
        return grid if f == 0 else pltpu.roll(grid, NY, 1)

    models = (den, sus)
    own_columns = [[models[f][:, j, :] for j in range(W)] for f in range(2)]
    b1[my] = forward(own_columns[0], 0) + forward(own_columns[1], 1)

    M[...] = jnp.zeros(M.shape, f32)
    F[...] = jnp.zeros(F.shape, f32)
    A[...] = jnp.zeros(A.shape, f32)
    CFX[...] = jnp.zeros(CFX.shape, f32)
    SH[...] = jnp.zeros(SH.shape, f32)
    CH[...] = jnp.zeros(CH.shape, f32)
    for f in range(2):
        for j in range(W):
            M[f, j + 1, 1 : R + 1, :] = own_columns[f][j]
        SH[0, f, 0:W, :] = models[f][R - 1]
        SH[1, f, 0:W, :] = models[f][0]
        SH[2, f, 0:R, :] = own_columns[f][W - 1]
        SH[3, f, 0:R, :] = own_columns[f][0]
        SH[4, f, 0:1, :] = models[f][R - 1, 0:1, :]
        SH[5, f, 0:1, :] = models[f][0, W - 1 : W, :]
    cellb[mx] = cell[...]
    lineb[mx] = line[...]
    obsb[mx] = obs[...]
    wgtb[mx] = wgt[...]

    pl.semaphore_wait(barrier, len(partners))

    def copy(src, dst, ssem, rsem, where):
        return pltpu.make_async_remote_copy(
            src_ref=src, dst_ref=dst, send_sem=ssem, recv_sem=rsem,
            device_id=where, device_id_type=MESH,
        )

    pending = []

    def share(buf, ssem, rsem, along_y):
        size, mine = (C, my) if along_y else (G, mx)
        for d, where in enumerate(ycast if along_y else xcast):
            one = copy(buf.at[mine], buf.at[mine], ssem.at[d], rsem.at[mine], where)
            one.start()
            pending.append(one)

    def arrived(buf, ssem, rsem, along_y):
        size, mine = (C, my) if along_y else (G, mx)
        for d in range(1, size):
            src = lax.rem(mine + d, size)
            copy(
                buf.at[src], buf.at[src], ssem.at[0], rsem.at[src],
                (ycast if along_y else xcast)[0],
            ).wait_recv()

    share(b1, s_b1, r_b1, True)
    station_bufs = (cellb, lineb, obsb, wgtb)
    for n, buf in enumerate(station_bufs):
        share(buf, s_st.at[n], r_st.at[n], False)
    halo_targets = [at(1, 0), at(-1, 0), at(0, 1), at(0, -1), at(1, -1), at(-1, 1)]
    halos = []
    for n, where in enumerate(halo_targets):
        one = copy(SH.at[n], RH.at[n], s_h.at[n], r_h.at[n], where)
        one.start()
        halos.append(one)
        pending.append(one)

    for n, buf in enumerate(station_bufs):
        arrived(buf, s_st.at[n], r_st.at[n], False)

    def spread_out(buf):
        return jnp.concatenate([buf[g, f : f + 1, :] for g in range(G) for f in range(2)], axis=1)

    field_of = (iota((1, ST), 1) // own) % 2
    cells = spread_out(cellb)
    lines = spread_out(lineb)
    observed = spread_out(obsb)
    weight = spread_out(wgtb)
    at_x = cells // NY
    at_y = cells - at_x * NY
    key_lane = (at_x % xp) * V + field_of * NY + at_y
    key_row = at_x // xp
    OY[...] = jnp.where(iota((128, ST), 0) == key_lane, 1.0, 0.0).astype(bf16)
    OX[...] = jnp.where(iota((Q, ST), 0) == key_row, 1.0, 0.0)
    OHI[...] = jnp.where(iota((2 * HIGH, ST), 0) == field_of * HIGH + lines // LOW, 1.0, 0.0)
    OLO[...] = jnp.where(iota((LOW, ST), 0) == lines % LOW, 1.0, 0.0).astype(bf16)
    counts = lax.dot_general(OHI[...].astype(bf16), OLO[...], NT, preferred_element_type=f32)
    per_line = 1.0 / jnp.maximum(counts, 1.0)

    def by_row(mask, v):
        return jnp.concatenate([(mask * p.astype(f32)).astype(bf16) for p in split3(v)], axis=0)

    def project(v):
        sums = lax.dot_general(by_row(OHI[...], v), OLO[...], NT, preferred_element_type=f32)
        means = thirds(sums) * per_line
        parts = jnp.concatenate(split3(means), axis=0)
        back = lax.dot_general(parts, OLO[...], NN, preferred_element_type=f32)
        return jnp.sum(thirds(back) * OHI[...], axis=0, keepdims=True)

    def at_stations(grid):
        parts = jnp.concatenate(split3(grid), axis=0)
        back = lax.dot_general(parts, OY[...], NN, preferred_element_type=f32)
        return jnp.sum(thirds(back) * OX[...], axis=0, keepdims=True)

    arrived(b1, s_b1, r_b1, True)
    partial = b1[0]
    for n in range(1, C):
        partial = partial + b1[n]
    b2[mx] = partial
    share(b2, s_b2, r_b2, False)

    for one in halos:
        one.wait_recv()
    for f in range(2):
        for j in range(W):
            M[f, j + 1, 0:1, :] = RH[0, f, j : j + 1, :]
            M[f, j + 1, R + 1 : R + 2, :] = RH[1, f, j : j + 1, :]
        M[f, 0, 1 : R + 1, :] = RH[2, f, 0:R, :]
        M[f, W + 1, 1 : R + 1, :] = RH[3, f, 0:R, :]
        M[f, W + 1, 0:1, :] = RH[4, f, 0:1, :]
        M[f, 0, R + 1 : R + 2, :] = RH[5, f, 0:1, :]
    mask_z = (iota((1, K), 1) < K - 1).astype(f32)

    def diffs(ref, f, c, row, count, global_x, global_y):
        base = ref[f, c, row : row + count, :]
        up = ref[f, c, row + 1 : row + 1 + count, :]
        right = ref[f, c + 1, row : row + count, :]
        keep_x = (global_x < NX - 1).astype(f32)
        keep_y = (global_y < NY - 1).astype(f32)
        return (
            (up - base) * keep_x,
            (right - base) * keep_y,
            (pltpu.roll(base, K - 1, 1) - base) * mask_z,
        )

    gx_rim = x0 - 1 + iota((16, K), 0)
    before = [None, None]
    for c in range(W + 1):
        gy_rim = y0 - 1 + c + jnp.zeros((16, K), jnp.int32)
        a = diffs(M, 0, c, 0, 16, gx_rim, gy_rim)
        b = diffs(M, 1, c, 0, 16, gx_rim, gy_rim)
        valid = ((gx_rim >= 0) & (gy_rim >= 0)).astype(f32)
        t = tuple(part * valid for part in cross(a, b))
        keep_x = (gx_rim < NX - 1).astype(f32)
        keep_y = (gy_rim < NY - 1).astype(f32)
        for f, force in enumerate((cross(b, t), cross(t, a))):
            fx, fy, fz = force[0] * keep_x, force[1] * keep_y, force[2] * mask_z
            if c > 0:
                d = before[f] - fy - fx + pltpu.roll(fz, 1, 1) - fz
                result = pltpu.roll(d, 15, 0)[0:R] + fx[0:R]
                CFX[f, c - 1, 0:R, :] = result
                cf_out[f, :, c - 1, :] = result
                CH[0, f, c - 1 : c, :] = result[0:1]
                if c == 1:
                    CH[1, f, 0:R, :] = result
            before[f] = fy
    force_halos = []
    for n, where in enumerate((at(-1, 0), at(0, -1))):
        one = copy(CH.at[n], CR.at[n], s_c.at[n], r_c.at[n], where)
        one.start()
        force_halos.append(one)
        pending.append(one)

    arrived(b2, s_b2, r_b2, False)
    grid = b2[0]
    for n in range(1, G):
        grid = grid + b2[n]

    misfit = at_stations(grid) - observed
    residual = misfit - project(misfit)
    weighted = weight * residual
    wrs[...] = weighted
    source = weight * weighted
    source = source - project(source)
    S = thirds(
        lax.dot_general(by_row(OX[...], source), OY[...], NT, preferred_element_type=f32)
    )

    for one in force_halos:
        one.wait_recv()
    for f in range(2):
        for j in range(W):
            CFX[f, j, R : R + 1, :] = CR[0, f, j : j + 1, :]
        CFX[f, W, 0:R, :] = CR[1, f, 0:R, :]

    for f in range(2):
        S_f = jnp.where(in_y, S if f == 0 else pltpu.roll(S, 128 - NY, 1), 0.0)
        A[f, 8 : 8 + Q, :] = S_f
        for j in range(W + 1):
            now = A[f, 7 : 7 + Q + 8, :]
            later = A[f, 8 : 8 + Q + 8, :]
            for c in range(xp):
                turn = (4 - j + 128 - c * V) % 128
                first = now if turn == 0 else pltpu.roll(now, turn, 1)
                second = later if turn == 0 else pltpu.roll(later, turn, 1)
                value = first if c == 0 else jnp.where(lane < 128 - c * V, first, second)
                high, low = split2(value)
                rows = pl.ds(8 - xp + c, Q + 8, stride=xp) if xp > 1 else pl.ds(7, Q + 8)
                F[f, j, 0, rows, :] = high.astype(f32)
                F[f, j, 1, rows, :] = low.astype(f32)
        for j in range(W + 1):
            for h in range(2):
                for n in range(nch):
                    RS[f, (h * (W + 1) + j) * 16 : (h * (W + 1) + j + 1) * 16, n * 128 : (n + 1) * 128] = F[
                        f, j, h, n * xp : n * xp + 16, :
                    ].astype(bf16)
        D = lax.dot_general(RS[f], E2[f], NT, preferred_element_type=f32)
        half = (W + 1) * 16
        D = D[:half] + D[half:]
        D = D[:, :K] + D[:, K:]
        for j in range(W + 1):
            piece = D[j * 16 : (j + 1) * 16]
            GE[f, j, 0:16, :] = piece + coupling * CFX[f, j]
            if j < W:
                dg_out[f, :, j, :] = piece[0:R]

    g_columns = [[GE[f, j, 0:R, :] for j in range(W)] for f in range(2)]
    c1[my] = forward(g_columns[0], 0) + forward(g_columns[1], 1)
    share(c1, s_c1, r_c1, True)

    sub16 = iota((16, K), 0)
    own_peak = functools.reduce(
        jnp.maximum, [jnp.abs(g_columns[f][j]) for f in range(2) for j in range(W)]
    )
    rim_peak = functools.reduce(
        jnp.maximum,
        [jnp.where(sub16 <= R, jnp.abs(GE[f, j, 0:16, :]), 0.0) for f in range(2) for j in range(W + 1)],
    )
    own_peak = largest(own_peak) + 1e-06
    scale = largest(rim_peak) + 1e-06
    for f in range(2):
        for j in range(W + 1):
            GE[f, j, 0:16, :] = GE[f, j, 0:16, :] / scale
    gx_own = x0 + iota((R, K), 0)
    powers = [jnp.zeros((R, K), f32) for _ in range(5)]
    for j in range(W):
        gy_own = y0 + j + jnp.zeros((R, K), jnp.int32)
        a = diffs(M, 0, j + 1, 1, R, gx_own, gy_own)
        b = diffs(M, 1, j + 1, 1, R, gx_own, gy_own)
        da = diffs(GE, 0, j, 0, R, gx_own, gy_own)
        db = diffs(GE, 1, j, 0, R, gx_own, gy_own)
        u = cross(a, b)
        v = tuple(p + q for p, q in zip(cross(da, b), cross(a, db)))
        w = cross(da, db)
        powers[0] += dot3(u, u)
        powers[1] -= 2.0 * dot3(u, v)
        powers[2] += dot3(v, v) + 2.0 * dot3(u, w)
        powers[3] -= 2.0 * dot3(v, w)
        powers[4] += dot3(w, w)
    scalars = [own_peak, scale] + [total(p) for p in powers]
    lane8 = iota((8, 128), 1)
    message = jnp.zeros((8, 128), f32)
    for n, value in enumerate(scalars):
        message = jnp.where(lane8 == n, value, message)
    s1[my] = message
    share(s1, s_s1, r_s1, True)

    arrived(c1, s_c1, r_c1, True)
    partial = c1[0]
    for n in range(1, C):
        partial = partial + c1[n]
    c2[mx] = partial
    share(c2, s_c2, r_c2, False)
    arrived(s1, s_s1, r_s1, True)
    s2[mx] = jnp.concatenate([s1[n, 0:1, :] for n in range(C)], axis=0)
    share(s2, s_s2, r_s2, False)

    chunk = 2 * own
    mine = wrs[0:1, pl.ds(pl.multiple_of(mx * chunk, 128), chunk)]
    for f in range(2):
        wr_out[f : f + 1, :] = mine[:, f * own : (f + 1) * own]

    arrived(c2, s_c2, r_c2, False)
    grid = c2[0]
    for n in range(1, G):
        grid = grid + c2[n]
    image = at_stations(grid)
    change = image - project(image)

    arrived(s2, s_s2, r_s2, False)
    table = jnp.concatenate([s2[n] for n in range(G)], axis=0)
    peak = jnp.max(table[:, 0:1], axis=0, keepdims=True)
    change = change / peak
    sub_t = iota((T, 128), 0)
    step_rows = jnp.zeros((T, 128), f32)
    step_lanes = jnp.zeros((1, 128), f32)
    for k in range(T):
        step_rows = jnp.where(sub_t == k, steps[k], step_rows)
        step_lanes = jnp.where(lane == k, steps[k], step_lanes)
    moved = weight * (residual - step_rows[:, 0:1] * change)
    data = 0.5 * jnp.sum(moved * moved, axis=1, keepdims=True)
    data = jnp.sum(jnp.where(iota((T, 128), 1) == sub_t, data, 0.0), axis=0, keepdims=True)
    tau = step_lanes * (table[:, 1:2] / peak)
    energy = table[:, 6:7] * tau
    for n in (5, 4, 3):
        energy = (energy + table[:, n : n + 1]) * tau
    energy = energy + table[:, 2:3]
    energy = 0.5 * jnp.sum(energy, axis=0, keepdims=True)
    values = (data + coupling * energy) / (2 * total_stations)
    tv_out[...] = values[:, 0:T]

    for one in pending:
        one.wait_send()


def body(G, C, density, susceptibility, station_cell, station_line, observed, data_weight, trial_steps):
    R, W, K = density.shape
    own = station_cell.shape[1]
    NX, NY = R * G, W * C
    V = 2 * NY
    xp = 128 // V
    Q = NX // xp
    N = (NX + 8) * V
    ST = 2 * own * G
    T = trial_steps.shape[0]
    vmem = pl.BlockSpec(memory_space=pltpu.VMEM)
    dma = pltpu.SemaphoreType.DMA
    scratch = [
        pltpu.VMEM((2, 2 * K, N), bf16),
        pltpu.VMEM((2, 2 * (W + 1) * 16, N), bf16),
        pltpu.VMEM((2, W + 1, 2, NX + 24, 128), f32),
        pltpu.VMEM((2, Q + 16, 128), f32),
        pltpu.VMEM((G, 2, own), jnp.int32),
        pltpu.VMEM((G, 2, own), jnp.int32),
        pltpu.VMEM((G, 2, own), f32),
        pltpu.VMEM((G, 2, own), f32),
        pltpu.VMEM((128, ST), bf16),
        pltpu.VMEM((Q, ST), f32),
        pltpu.VMEM((2 * HIGH, ST), f32),
        pltpu.VMEM((LOW, ST), bf16),
        pltpu.VMEM((1, ST), f32),
        pltpu.VMEM((C, Q, 128), f32),
        pltpu.VMEM((G, Q, 128), f32),
        pltpu.VMEM((C, Q, 128), f32),
        pltpu.VMEM((G, Q, 128), f32),
        pltpu.VMEM((C, 8, 128), f32),
        pltpu.VMEM((G, C, 128), f32),
        pltpu.VMEM((2, W + 2, 24, K), f32),
        pltpu.VMEM((6, 2, 8, K), f32),
        pltpu.VMEM((6, 2, 8, K), f32),
        pltpu.VMEM((2, 2, 8, K), f32),
        pltpu.VMEM((2, 2, 8, K), f32),
        pltpu.VMEM((2, W + 1, 16, K), f32),
        pltpu.VMEM((2, W + 1, 24, K), f32),
        dma((4, G)), dma((4, G)),
        dma((6,)), dma((6,)),
        dma((2,)), dma((2,)),
        dma((C,)), dma((C,)),
        dma((G,)), dma((G,)),
        dma((C,)), dma((C,)),
        dma((G,)), dma((G,)),
        dma((C,)), dma((C,)),
        dma((G,)), dma((G,)),
    ]
    out = pl.pallas_call(
        functools.partial(kernel, G, C),
        out_shape=(
            jax.ShapeDtypeStruct((2, R, W, K), f32),
            jax.ShapeDtypeStruct((2, R, W, K), f32),
            jax.ShapeDtypeStruct((2, own), f32),
            jax.ShapeDtypeStruct((1, T), f32),
        ),
        in_specs=[vmem] * 6 + [pl.BlockSpec(memory_space=pltpu.SMEM)],
        out_specs=(vmem,) * 4,
        scratch_shapes=scratch,
        compiler_params=pltpu.CompilerParams(
            collective_id=0, has_side_effects=True, vmem_limit_bytes=56 * 1024 * 1024
        ),
    )(density, susceptibility, station_cell, station_line, observed, data_weight, trial_steps)
    return out[0], out[1], out[2], out[3].reshape(-1)


def solution(mesh):
    placed = (
        P("gx", "gy", None),
        P("gx", "gy", None),
        P(None, "gx"),
        P(None, "gx"),
        P(None, "gx"),
        P(None, "gx"),
        P(),
    )
    return jax.shard_map(
        functools.partial(body, mesh.shape["gx"], mesh.shape["gy"]),
        mesh=mesh,
        in_specs=placed,
        out_specs=(P(None, "gx", "gy", None), P(None, "gx", "gy", None), P(None, "gx"), P()),
        check_vma=False,
    )
```

time: 426 us -> 30.5 us (0.07)
  blocking collectives: 155 us -> 0 us
  matrix products: 140 us -> 0 us
  waiting for transfers between devices: 33.6 us -> 0 us
  other arithmetic: 28.7 us -> 0 us
  Pallas kernels: 0 us -> 26.3 us
  between operations: 26 us -> 0.65 us
  starting transfers between devices: 16 us -> 0 us
  local copies, waits for them, and re-layouts: 15.6 us -> 3.23 us
  loops' own time: 9.71 us -> 0 us
    dot_general x198 -> x0, matrix products: 140 us -> none  [the longest x128 97.5 us: forward_cell_turn(): jnp.dot(kernel_tile(field, block_x[field], block_y[field], cell_x, cell_y...]
    psum x6 -> x0, blocking collectives: 95 us -> none  [the longest x1 40 us: body(): lax.psum(jnp.stack(shares), ('gx', 'gy')) / (2 * total_stations)]
    pmax x1 -> x0, blocking collectives: 39.4 us -> none  [body(): peak = lax.pmax(jnp.max(jnp.abs(gradient)), ('gx', 'gy')) + 1e-06]
    unnamed x2 -> x0, waiting for transfers between devices: 33.6 us -> none
    pallas_call x0 -> x1, Pallas kernels: none -> 26.3 us  [body(): pl.pallas_call(functools.partial(kernel, G, C), out_shape=(jax.ShapeDtype...]
    all_gather x2 -> x0, blocking collectives: 20.1 us -> none  [column_data(): lax.all_gather(fields, 'gx', axis=1, tiled=True)]
    ppermute x8 -> x0, starting transfers between devices: 16 us -> none  [the longest x4 10.8 us: extended_2(): lax.ppermute(lax.slice_in_dim(block, block.shape[dim] - width, None, axis...]
    another operation x19 -> x0, loops' own time: 9.71 us -> none  [the longest x1 5.48 us: adjoint_part(): lax.map(adjoint_cell_turn, jnp.arange(cells // cell_block, dtype=jnp.int32))]
  transfers between devices with their start and end apart: 9 -> 0, of which waited for: 1 -> 0; matrix products, arithmetic and copies ran while one was open for 40% -> 0% of each run, Pallas kernels for 0% -> 0%
where the time goes in v1:
time: 30.5 us; the launch traced here: 30.2 us
  Pallas kernels  26.3 us (86%)
  local copies, waits for them, and re-layouts  3.23 us (11%)
  between operations  0.65 us (2%)
    pallas_call x1, Pallas kernels, body(): pl.pallas_call(functools.partial(kernel, G, C), out_shape=(jax.ShapeDtype...  26.3 us
    unnamed x10, local copies, waits for them, and re-layouts  3.23 us

profile of v1, /device:TPU:0, one launch (start us, length us, event | category | flops | bytes accessed | tf_op | source)
XLA Modules:
  0.0 30.2 jit_solution(10439282248967987825)
XLA Ops:
  0.6 26.3 %shard_map.102 = (f32[2,8,4,128]{3,2,1,0:T(4,128)}, f32[2,8,4,128]{3,2,1,0:T(4,128)}, f32[2,256]{1,0:T(2,128)}, f32[1,8]{1,0:T(1,128)}) custom-call(f32[8,4,128]{2,1,0:T(4,128)} %den.1, f32[8,4,128]{2,1,0:T(4,128)} %sus.1, s32[2,256]{1,0:T(2,128)} %cell.1, s32[2,256]{1,0:T(2,128)} %line.1, f32[2,256]{1,0:T(2,128)} %obs.1, f32[2,256]{1,0:T(2,128)} %wgt.1, f32[8]{0:T(128)} %steps.1), custom_call_target="tpu_custom_call" | custom-call | tf_op jit(solution)/shard_map/pallas_call | solution.py:491
  27.0 0.0 copy-start
  27.0 1.4 %copy.15 = f32[2,8,4,128]{3,2,1,0:T(4,128)} copy(f32[2,8,4,128]{3,2,1,0:T(4,128)} %get-tuple-element.16) | data formatting | bytes 65536
  28.4 0.0 copy-done
  28.4 0.0 copy-start.1
  28.4 0.6 %copy.16 = f32[2,8,4,128]{3,2,1,0:T(4,128)} copy(f32[2,8,4,128]{3,2,1,0:T(4,128)S(1)} %copy-done) | data formatting | bytes 65536
  29.0 0.1 copy-done.1
  29.0 0.0 copy-start.2
  29.0 0.6 %copy.17 = f32[2,256]{1,0:T(2,128)} copy(f32[2,256]{1,0:T(2,128)S(1)} %copy-done.1) | data formatting | bytes 4096
  29.6 0.1 copy-done.2
  29.7 0.5 %copy.18 = f32[8]{0:T(128)} copy(f32[8]{0:T(128)S(1)} %bitcast.1) | data formatting | bytes 64
Async XLA Ops:
  27.0 1.4 %copy-start = (f32[2,8,4,128]{3,2,1,0:T(4,128)S(1)}, f32[2,8,4,128]{3,2,1,0:T(4,128)}, u32[]{:S(2)}) copy-start(f32[2,8,4,128]{3,2,1,0:T(4,128)} %get-tuple-element.17) | copy-start | bytes 98308
  28.4 0.7 %copy-start.1 = (f32[2,256]{1,0:T(2,128)S(1)}, f32[2,256]{1,0:T(2,128)}, u32[]{:S(2)}) copy-start(f32[2,256]{1,0:T(2,128)} %get-tuple-element.18) | copy-start | bytes 6148
  29.0 0.7 %copy-start.2 = (f32[1,8]{1,0:T(1,128)S(1)}, f32[1,8]{1,0:T(1,128)}, u32[]{:S(2)}) copy-start(f32[1,8]{1,0:T(1,128)} %get-tuple-element.11) | copy-start | bytes 100

commit v2 on v1

--- a/solution.py
+++ b/solution.py
@@ -9,6 +9,7 @@
 
 LINES = 256
 LOW = 32
+CORES = 2
 HIGH = LINES // LOW
 
 cell_depth = 2.0
@@ -60,14 +61,14 @@
 
 
 def kernel(
-    G, C, den, sus, cell, line, obs, wgt, steps,
+    G, C, den_in, sus_in, cell_in, line_in, obs_in, wgt_in, steps_in,
     dg_out, cf_out, wr_out, tv_out,
-    E2, RS, F, A, cellb, lineb, obsb, wgtb, OY, OX, OHI, OLO, wrs,
+    den, sus, steps, s_in, E2, RS, F, A, cellb, lineb, obsb, wgtb, OY, OX, OHI, OLO, wrs,
     b1, b2, c1, c2, s1, s2, M, SH, RH, CH, CR, CFX, GE,
     s_st, r_st, s_h, r_h, s_c, r_c, s_b1, r_b1, s_b2, r_b2, s_c1, r_c1, s_c2, r_c2, s_s1, r_s1, s_s2, r_s2,
 ):
     R, W, K = den.shape
-    own = cell.shape[1]
+    own = cell_in.shape[1]
     NX, NY = R * G, W * C
     V = 2 * NY
     xp = 128 // V
@@ -86,13 +87,49 @@
     def at(dx, dy):
         return (lax.rem(mx + dx + G, G), lax.rem(my + dy + C, C))
 
-    ycast = [at(0, d) for d in range(1, C)]
+    Z = C // CORES
+    chip, core = my // CORES, lax.rem(my, CORES)
+    zcast = [at(0, CORES * d) for d in range(1, Z)]
     xcast = [at(d, 0) for d in range(1, G)]
-    diagonal = [at(1, -1), at(-1, 1)]
+    gcast = xcast + [
+        (lax.rem(mx + d, G), chip * CORES + lax.rem(core + e, CORES)) for e in range(1, CORES) for d in range(G)
+    ]
+    groups = {
+        "z": (zcast, chip, [lax.rem(chip + d, Z) for d in range(1, Z)]),
+        "x": (xcast, mx, [lax.rem(mx + d, G) for d in range(1, G)]),
+        "g": (
+            gcast,
+            mx * CORES + core,
+            [lax.rem(mx + d, G) * CORES + core for d in range(1, G)]
+            + [
+                lax.rem(mx + d, G) * CORES + lax.rem(core + e, CORES)
+                for e in range(1, CORES)
+                for d in range(G)
+            ],
+        ),
+    }
+    slot = mx * CORES + core
     barrier = pltpu.get_barrier_semaphore()
-    partners = ycast + xcast + diagonal
+    partners = zcast + gcast + [at(0, 1), at(0, -1), at(1, -1), at(-1, 1)]
     for where in partners:
         pl.semaphore_signal(barrier, inc=1, device_id=where, device_id_type=MESH)
+
+    loads = [
+        pltpu.make_async_copy(src, dst, s_in.at[n])
+        for n, (src, dst) in enumerate(
+            (
+                (den_in, den),
+                (sus_in, sus),
+                (cell_in, cellb.at[mx]),
+                (line_in, lineb.at[mx]),
+                (obs_in, obsb.at[mx]),
+                (wgt_in, wgtb.at[mx]),
+                (steps_in, steps),
+            )
+        )
+    ]
+    for one in loads:
+        one.start()
 
     lane = iota((1, 128), 1)
 
@@ -139,9 +176,11 @@
         grid = jnp.where(in_y, grid, 0.0)
         return grid if f == 0 else pltpu.roll(grid, NY, 1)
 
+    for one in loads[:2]:
+        one.wait()
     models = (den, sus)
     own_columns = [[models[f][:, j, :] for j in range(W)] for f in range(2)]
-    b1[my] = forward(own_columns[0], 0) + forward(own_columns[1], 1)
+    b1[chip] = forward(own_columns[0], 0) + forward(own_columns[1], 1)
 
     M[...] = jnp.zeros(M.shape, f32)
     F[...] = jnp.zeros(F.shape, f32)
@@ -149,6 +188,7 @@
     CFX[...] = jnp.zeros(CFX.shape, f32)
     SH[...] = jnp.zeros(SH.shape, f32)
     CH[...] = jnp.zeros(CH.shape, f32)
+    s2[slot] = jnp.zeros(s2.shape[1:], f32)
     for f in range(2):
         for j in range(W):
             M[f, j + 1, 1 : R + 1, :] = own_columns[f][j]
@@ -158,10 +198,8 @@
         SH[3, f, 0:R, :] = own_columns[f][0]
         SH[4, f, 0:1, :] = models[f][R - 1, 0:1, :]
         SH[5, f, 0:1, :] = models[f][0, W - 1 : W, :]
-    cellb[mx] = cell[...]
-    lineb[mx] = line[...]
-    obsb[mx] = obs[...]
-    wgtb[mx] = wgt[...]
+    for one in loads[2:]:
+        one.wait()
 
     pl.semaphore_wait(barrier, len(partners))
 
@@ -173,26 +211,22 @@
 
     pending = []
 
-    def share(buf, ssem, rsem, along_y):
-        size, mine = (C, my) if along_y else (G, mx)
-        for d, where in enumerate(ycast if along_y else xcast):
+    def share(buf, ssem, rsem, group):
+        targets, mine, _ = groups[group]
+        for d, where in enumerate(targets):
             one = copy(buf.at[mine], buf.at[mine], ssem.at[d], rsem.at[mine], where)
             one.start()
             pending.append(one)
 
-    def arrived(buf, ssem, rsem, along_y):
-        size, mine = (C, my) if along_y else (G, mx)
-        for d in range(1, size):
-            src = lax.rem(mine + d, size)
-            copy(
-                buf.at[src], buf.at[src], ssem.at[0], rsem.at[src],
-                (ycast if along_y else xcast)[0],
-            ).wait_recv()
-
-    share(b1, s_b1, r_b1, True)
+    def arrived(buf, ssem, rsem, group):
+        targets, _, sources = groups[group]
+        for src in sources:
+            copy(buf.at[src], buf.at[src], ssem.at[0], rsem.at[src], targets[0]).wait_recv()
+
+    share(b1, s_b1, r_b1, "z")
     station_bufs = (cellb, lineb, obsb, wgtb)
     for n, buf in enumerate(station_bufs):
-        share(buf, s_st.at[n], r_st.at[n], False)
+        share(buf, s_st.at[n], r_st.at[n], "x")
     halo_targets = [at(1, 0), at(-1, 0), at(0, 1), at(0, -1), at(1, -1), at(-1, 1)]
     halos = []
     for n, where in enumerate(halo_targets):
@@ -202,7 +236,7 @@
         pending.append(one)
 
     for n, buf in enumerate(station_bufs):
-        arrived(buf, s_st.at[n], r_st.at[n], False)
+        arrived(buf, s_st.at[n], r_st.at[n], "x")
 
     def spread_out(buf):
         return jnp.concatenate([buf[g, f : f + 1, :] for g in range(G) for f in range(2)], axis=1)
@@ -238,12 +272,12 @@
         back = lax.dot_general(parts, OY[...], NN, preferred_element_type=f32)
         return jnp.sum(thirds(back) * OX[...], axis=0, keepdims=True)
 
-    arrived(b1, s_b1, r_b1, True)
+    arrived(b1, s_b1, r_b1, "z")
     partial = b1[0]
-    for n in range(1, C):
+    for n in range(1, Z):
         partial = partial + b1[n]
-    b2[mx] = partial
-    share(b2, s_b2, r_b2, False)
+    b2[slot] = partial
+    share(b2, s_b2, r_b2, "g")
 
     for one in halos:
         one.wait_recv()
@@ -297,9 +331,9 @@
         force_halos.append(one)
         pending.append(one)
 
-    arrived(b2, s_b2, r_b2, False)
+    arrived(b2, s_b2, r_b2, "g")
     grid = b2[0]
-    for n in range(1, G):
+    for n in range(1, CORES * G):
         grid = grid + b2[n]
 
     misfit = at_stations(grid) - observed
@@ -351,8 +385,8 @@
                 dg_out[f, :, j, :] = piece[0:R]
 
     g_columns = [[GE[f, j, 0:R, :] for j in range(W)] for f in range(2)]
-    c1[my] = forward(g_columns[0], 0) + forward(g_columns[1], 1)
-    share(c1, s_c1, r_c1, True)
+    c1[chip] = forward(g_columns[0], 0) + forward(g_columns[1], 1)
+    share(c1, s_c1, r_c1, "z")
 
     sub16 = iota((16, K), 0)
     own_peak = functools.reduce(
@@ -388,33 +422,33 @@
     message = jnp.zeros((8, 128), f32)
     for n, value in enumerate(scalars):
         message = jnp.where(lane8 == n, value, message)
-    s1[my] = message
-    share(s1, s_s1, r_s1, True)
-
-    arrived(c1, s_c1, r_c1, True)
+    s1[chip] = message
+    share(s1, s_s1, r_s1, "z")
+
+    arrived(c1, s_c1, r_c1, "z")
     partial = c1[0]
-    for n in range(1, C):
+    for n in range(1, Z):
         partial = partial + c1[n]
-    c2[mx] = partial
-    share(c2, s_c2, r_c2, False)
-    arrived(s1, s_s1, r_s1, True)
-    s2[mx] = jnp.concatenate([s1[n, 0:1, :] for n in range(C)], axis=0)
-    share(s2, s_s2, r_s2, False)
+    c2[slot] = partial
+    share(c2, s_c2, r_c2, "g")
+    arrived(s1, s_s1, r_s1, "z")
+    s2[slot, 0:Z, :] = jnp.concatenate([s1[n, 0:1, :] for n in range(Z)], axis=0)
+    share(s2, s_s2, r_s2, "g")
 
     chunk = 2 * own
     mine = wrs[0:1, pl.ds(pl.multiple_of(mx * chunk, 128), chunk)]
     for f in range(2):
         wr_out[f : f + 1, :] = mine[:, f * own : (f + 1) * own]
 
-    arrived(c2, s_c2, r_c2, False)
+    arrived(c2, s_c2, r_c2, "g")
     grid = c2[0]
-    for n in range(1, G):
+    for n in range(1, CORES * G):
         grid = grid + c2[n]
     image = at_stations(grid)
     change = image - project(image)
 
-    arrived(s2, s_s2, r_s2, False)
-    table = jnp.concatenate([s2[n] for n in range(G)], axis=0)
+    arrived(s2, s_s2, r_s2, "g")
+    table = jnp.concatenate([s2[n] for n in range(CORES * G)], axis=0)
     peak = jnp.max(table[:, 0:1], axis=0, keepdims=True)
     change = change / peak
     sub_t = iota((T, 128), 0)
@@ -439,6 +473,14 @@
         one.wait_send()
 
 
+def deliver(*refs):
+    moves = [pltpu.make_async_copy(refs[n], refs[4 + n], refs[8].at[n]) for n in range(4)]
+    for one in moves:
+        one.start()
+    for one in moves:
+        one.wait()
+
+
 def body(G, C, density, susceptibility, station_cell, station_line, observed, data_weight, trial_steps):
     R, W, K = density.shape
     own = station_cell.shape[1]
@@ -451,7 +493,12 @@
     T = trial_steps.shape[0]
     vmem = pl.BlockSpec(memory_space=pltpu.VMEM)
     dma = pltpu.SemaphoreType.DMA
+    Z = C // CORES
     scratch = [
+        pltpu.VMEM((R, W, K), f32),
+        pltpu.VMEM((R, W, K), f32),
+        pltpu.SMEM((T,), f32),
+        dma((7,)),
         pltpu.VMEM((2, 2 * K, N), bf16),
         pltpu.VMEM((2, 2 * (W + 1) * 16, N), bf16),
         pltpu.VMEM((2, W + 1, 2, NX + 24, 128), f32),
@@ -465,12 +512,12 @@
         pltpu.VMEM((2 * HIGH, ST), f32),
         pltpu.VMEM((LOW, ST), bf16),
         pltpu.VMEM((1, ST), f32),
-        pltpu.VMEM((C, Q, 128), f32),
-        pltpu.VMEM((G, Q, 128), f32),
-        pltpu.VMEM((C, Q, 128), f32),
-        pltpu.VMEM((G, Q, 128), f32),
-        pltpu.VMEM((C, 8, 128), f32),
-        pltpu.VMEM((G, C, 128), f32),
+        pltpu.VMEM((Z, Q, 128), f32),
+        pltpu.VMEM((CORES * G, Q, 128), f32),
+        pltpu.VMEM((Z, Q, 128), f32),
+        pltpu.VMEM((CORES * G, Q, 128), f32),
+        pltpu.VMEM((Z, 8, 128), f32),
+        pltpu.VMEM((CORES * G, -(-Z // 8) * 8, 128), f32),
         pltpu.VMEM((2, W + 2, 24, K), f32),
         pltpu.VMEM((6, 2, 8, K), f32),
         pltpu.VMEM((6, 2, 8, K), f32),
@@ -481,28 +528,36 @@
         dma((4, G)), dma((4, G)),
         dma((6,)), dma((6,)),
         dma((2,)), dma((2,)),
-        dma((C,)), dma((C,)),
-        dma((G,)), dma((G,)),
-        dma((C,)), dma((C,)),
-        dma((G,)), dma((G,)),
-        dma((C,)), dma((C,)),
-        dma((G,)), dma((G,)),
+        dma((Z,)), dma((Z,)),
+        dma((CORES * G,)), dma((CORES * G,)),
+        dma((Z,)), dma((Z,)),
+        dma((CORES * G,)), dma((CORES * G,)),
+        dma((Z,)), dma((Z,)),
+        dma((CORES * G,)), dma((CORES * G,)),
     ]
     out = pl.pallas_call(
         functools.partial(kernel, G, C),
         out_shape=(
-            jax.ShapeDtypeStruct((2, R, W, K), f32),
-            jax.ShapeDtypeStruct((2, R, W, K), f32),
-            jax.ShapeDtypeStruct((2, own), f32),
-            jax.ShapeDtypeStruct((1, T), f32),
+            pltpu.VMEM((2, R, W, K), f32),
+            pltpu.VMEM((2, R, W, K), f32),
+            pltpu.VMEM((2, own), f32),
+            pltpu.VMEM((1, T), f32),
         ),
-        in_specs=[vmem] * 6 + [pl.BlockSpec(memory_space=pltpu.SMEM)],
+        in_specs=[pl.BlockSpec(memory_space=pltpu.HBM)] * 7,
         out_specs=(vmem,) * 4,
         scratch_shapes=scratch,
         compiler_params=pltpu.CompilerParams(
-            collective_id=0, has_side_effects=True, vmem_limit_bytes=56 * 1024 * 1024
+            collective_id=0, has_side_effects=True, vmem_limit_bytes=60 * 1024 * 1024
         ),
     )(density, susceptibility, station_cell, station_line, observed, data_weight, trial_steps)
+    out = pl.pallas_call(
+        deliver,
+        out_shape=tuple(jax.ShapeDtypeStruct(x.shape, x.dtype) for x in out),
+        in_specs=[vmem] * 4,
+        out_specs=(pl.BlockSpec(memory_space=pltpu.HBM),) * 4,
+        scratch_shapes=[dma((4,))],
+        compiler_params=pltpu.CompilerParams(vmem_limit_bytes=1024 * 1024),
+    )(*out)
     return out[0], out[1], out[2], out[3].reshape(-1)
 
 

time: 30.5 us -> 26.5 us (0.87)
  local copies, waits for them, and re-layouts: 3.23 us -> 0 us
  Pallas kernels: 26.3 us -> 25.7 us
    unnamed x10 -> x0, local copies, waits for them, and re-layouts: 3.23 us -> none
    pallas_call x1 -> x2, Pallas kernels: 26.3 us -> 25.7 us  [the longest x1 25 us: body(): pl.pallas_call(functools.partial(kernel, G, C), out_shape=(pltpu.VMEM((2,...]
where the time goes in v2:
time: 26.5 us; the launch traced here: 26.3 us
  Pallas kernels  25.7 us (97%)
  between operations  0.64 us (2%)
    pallas_call x1, Pallas kernels, body(): pl.pallas_call(functools.partial(kernel, G, C), out_shape=(pltpu.VMEM((2,...  25 us
    pallas_call x1, Pallas kernels, body(): pl.pallas_call(deliver, out_shape=tuple((jax.ShapeDtypeStruct(x.shape, x....  0.67 us

profile of v2, /device:TPU:0, one launch (start us, length us, event | category | flops | bytes accessed | tf_op | source)
XLA Modules:
  0.0 26.3 jit_solution(12052503107039521870)
XLA Ops:
  0.6 25.0 %shard_map.102 = (f32[2,8,4,128]{3,2,1,0:T(4,128)S(1)}, f32[2,8,4,128]{3,2,1,0:T(4,128)S(1)}, f32[2,256]{1,0:T(2,128)S(1)}, f32[1,8]{1,0:T(1,128)S(1)}) custom-call(f32[8,4,128]{2,1,0:T(4,128)} %den_in.1, f32[8,4,128]{2,1,0:T(4,128)} %sus_in.1, s32[2,256]{1,0:T(2,128)} %cell_in.1, s32[2,256]{1,0:T(2,128)} %line_in.1, f32[2,256]{1,0:T(2,128)} %obs_in.1, ...), custom_call_target="tpu_custom_call" | custom-call | tf_op jit(solution)/shard_map/pallas_call | solution.py:538
  25.7 0.7 %shard_map.103 = (f32[2,8,4,128]{3,2,1,0:T(4,128)}, f32[2,8,4,128]{3,2,1,0:T(4,128)}, f32[2,256]{1,0:T(2,128)}, f32[1,8]{1,0:T(1,128)}) custom-call(f32[2,8,4,128]{3,2,1,0:T(4,128)S(1)} %get-tuple-element.12.refs_0_, f32[2,8,4,128]{3,2,1,0:T(4,128)S(1)} %get-tuple-element.13.refs_1_, f32[2,256]{1,0:T(2,128)S(1)} %get-tuple-element.14.refs_2_, ...), custom_call_target="tpu_custom_call" | custom-call | tf_op jit(solution)/shard_map/pallas_call | solution.py:553

commit v3 on v2

--- a/solution.py
+++ b/solution.py
@@ -174,14 +174,42 @@
         row = jnp.sum(acc, axis=0, keepdims=True)
         grid = jnp.concatenate([row[:, q * 128 : (q + 1) * 128] for q in range(Q)], axis=0)
         grid = jnp.where(in_y, grid, 0.0)
-        return grid if f == 0 else pltpu.roll(grid, NY, 1)
+        return grid[: Q // 2] + pltpu.roll(grid[Q // 2 :], NY, 1)
 
     for one in loads[:2]:
         one.wait()
     models = (den, sus)
     own_columns = [[models[f][:, j, :] for j in range(W)] for f in range(2)]
-    b1[chip] = forward(own_columns[0], 0) + forward(own_columns[1], 1)
-
+    def copy(src, dst, ssem, rsem, where):
+        return pltpu.make_async_remote_copy(
+            src_ref=src, dst_ref=dst, send_sem=ssem, recv_sem=rsem,
+            device_id=where, device_id_type=MESH,
+        )
+
+    pending = []
+
+    def share(buf, ssem, rsem, group):
+        targets, mine, _ = groups[group]
+        for d, where in enumerate(targets):
+            one = copy(buf.at[mine], buf.at[mine], ssem.at[d], rsem.at[mine], where)
+            one.start()
+            pending.append(one)
+
+    def arrived(buf, ssem, rsem, group):
+        targets, _, sources = groups[group]
+        for src in sources:
+            copy(buf.at[src], buf.at[src], ssem.at[0], rsem.at[src], targets[0]).wait_recv()
+
+    b1[0, chip] = forward(own_columns[0], 0)
+    pl.semaphore_wait(barrier, len(partners))
+    share(b1.at[0], s_b1.at[0], r_b1.at[0], "z")
+    b1[1, chip] = forward(own_columns[1], 1)
+    share(b1.at[1], s_b1.at[1], r_b1.at[1], "z")
+    for one in loads[2:]:
+        one.wait()
+    station_bufs = (cellb, lineb, obsb, wgtb)
+    for n, buf in enumerate(station_bufs):
+        share(buf, s_st.at[n], r_st.at[n], "x")
     M[...] = jnp.zeros(M.shape, f32)
     F[...] = jnp.zeros(F.shape, f32)
     A[...] = jnp.zeros(A.shape, f32)
@@ -198,35 +226,6 @@
         SH[3, f, 0:R, :] = own_columns[f][0]
         SH[4, f, 0:1, :] = models[f][R - 1, 0:1, :]
         SH[5, f, 0:1, :] = models[f][0, W - 1 : W, :]
-    for one in loads[2:]:
-        one.wait()
-
-    pl.semaphore_wait(barrier, len(partners))
-
-    def copy(src, dst, ssem, rsem, where):
-        return pltpu.make_async_remote_copy(
-            src_ref=src, dst_ref=dst, send_sem=ssem, recv_sem=rsem,
-            device_id=where, device_id_type=MESH,
-        )
-
-    pending = []
-
-    def share(buf, ssem, rsem, group):
-        targets, mine, _ = groups[group]
-        for d, where in enumerate(targets):
-            one = copy(buf.at[mine], buf.at[mine], ssem.at[d], rsem.at[mine], where)
-            one.start()
-            pending.append(one)
-
-    def arrived(buf, ssem, rsem, group):
-        targets, _, sources = groups[group]
-        for src in sources:
-            copy(buf.at[src], buf.at[src], ssem.at[0], rsem.at[src], targets[0]).wait_recv()
-
-    share(b1, s_b1, r_b1, "z")
-    station_bufs = (cellb, lineb, obsb, wgtb)
-    for n, buf in enumerate(station_bufs):
-        share(buf, s_st.at[n], r_st.at[n], "x")
     halo_targets = [at(1, 0), at(-1, 0), at(0, 1), at(0, -1), at(1, -1), at(-1, 1)]
     halos = []
     for n, where in enumerate(halo_targets):
@@ -248,8 +247,8 @@
     weight = spread_out(wgtb)
     at_x = cells // NY
     at_y = cells - at_x * NY
-    key_lane = (at_x % xp) * V + field_of * NY + at_y
-    key_row = at_x // xp
+    key_lane = (at_x % xp) * V + (at_x // (NX // 2)) * NY + at_y
+    key_row = field_of * (Q // 2) + (at_x // xp) % (Q // 2)
     OY[...] = jnp.where(iota((128, ST), 0) == key_lane, 1.0, 0.0).astype(bf16)
     OX[...] = jnp.where(iota((Q, ST), 0) == key_row, 1.0, 0.0)
     OHI[...] = jnp.where(iota((2 * HIGH, ST), 0) == field_of * HIGH + lines // LOW, 1.0, 0.0)
@@ -272,12 +271,26 @@
         back = lax.dot_general(parts, OY[...], NN, preferred_element_type=f32)
         return jnp.sum(thirds(back) * OX[...], axis=0, keepdims=True)
 
-    arrived(b1, s_b1, r_b1, "z")
-    partial = b1[0]
-    for n in range(1, Z):
-        partial = partial + b1[n]
-    b2[slot] = partial
-    share(b2, s_b2, r_b2, "g")
+    def pass_on(first, sends1, recvs1, second, sends2, recvs2, f):
+        arrived(first.at[f], sends1.at[f], recvs1.at[f], "z")
+        partial = first[f, 0]
+        for n in range(1, Z):
+            partial = partial + first[f, n]
+        second[f, slot] = partial
+        share(second.at[f], sends2.at[f], recvs2.at[f], "g")
+
+    def gathered(buf, sends, recvs):
+        halves = []
+        for f in range(2):
+            arrived(buf.at[f], sends.at[f], recvs.at[f], "g")
+            grid = buf[f, 0]
+            for n in range(1, CORES * G):
+                grid = grid + buf[f, n]
+            halves.append(grid)
+        return jnp.concatenate(halves, axis=0)
+
+    for f in range(2):
+        pass_on(b1, s_b1, r_b1, b2, s_b2, r_b2, f)
 
     for one in halos:
         one.wait_recv()
@@ -331,12 +344,7 @@
         force_halos.append(one)
         pending.append(one)
 
-    arrived(b2, s_b2, r_b2, "g")
-    grid = b2[0]
-    for n in range(1, CORES * G):
-        grid = grid + b2[n]
-
-    misfit = at_stations(grid) - observed
+    misfit = at_stations(gathered(b2, s_b2, r_b2)) - observed
     residual = misfit - project(misfit)
     weighted = weight * residual
     wrs[...] = weighted
@@ -354,8 +362,9 @@
         CFX[f, W, 0:R, :] = CR[1, f, 0:R, :]
 
     for f in range(2):
-        S_f = jnp.where(in_y, S if f == 0 else pltpu.roll(S, 128 - NY, 1), 0.0)
-        A[f, 8 : 8 + Q, :] = S_f
+        half_f = S[f * (Q // 2) : (f + 1) * (Q // 2)]
+        A[f, 8 : 8 + Q // 2, :] = jnp.where(in_y, half_f, 0.0)
+        A[f, 8 + Q // 2 : 8 + Q, :] = jnp.where(in_y, pltpu.roll(half_f, 128 - NY, 1), 0.0)
         for j in range(W + 1):
             now = A[f, 7 : 7 + Q + 8, :]
             later = A[f, 8 : 8 + Q + 8, :]
@@ -383,10 +392,10 @@
             GE[f, j, 0:16, :] = piece + coupling * CFX[f, j]
             if j < W:
                 dg_out[f, :, j, :] = piece[0:R]
+        c1[f, chip] = forward([GE[f, j, 0:R, :] for j in range(W)], f)
+        share(c1.at[f], s_c1.at[f], r_c1.at[f], "z")
 
     g_columns = [[GE[f, j, 0:R, :] for j in range(W)] for f in range(2)]
-    c1[chip] = forward(g_columns[0], 0) + forward(g_columns[1], 1)
-    share(c1, s_c1, r_c1, "z")
 
     sub16 = iota((16, K), 0)
     own_peak = functools.reduce(
@@ -425,12 +434,8 @@
     s1[chip] = message
     share(s1, s_s1, r_s1, "z")
 
-    arrived(c1, s_c1, r_c1, "z")
-    partial = c1[0]
-    for n in range(1, Z):
-        partial = partial + c1[n]
-    c2[slot] = partial
-    share(c2, s_c2, r_c2, "g")
+    for f in range(2):
+        pass_on(c1, s_c1, r_c1, c2, s_c2, r_c2, f)
     arrived(s1, s_s1, r_s1, "z")
     s2[slot, 0:Z, :] = jnp.concatenate([s1[n, 0:1, :] for n in range(Z)], axis=0)
     share(s2, s_s2, r_s2, "g")
@@ -440,11 +445,7 @@
     for f in range(2):
         wr_out[f : f + 1, :] = mine[:, f * own : (f + 1) * own]
 
-    arrived(c2, s_c2, r_c2, "g")
-    grid = c2[0]
-    for n in range(1, CORES * G):
-        grid = grid + c2[n]
-    image = at_stations(grid)
+    image = at_stations(gathered(c2, s_c2, r_c2))
     change = image - project(image)
 
     arrived(s2, s_s2, r_s2, "g")
@@ -512,10 +513,10 @@
         pltpu.VMEM((2 * HIGH, ST), f32),
         pltpu.VMEM((LOW, ST), bf16),
         pltpu.VMEM((1, ST), f32),
-        pltpu.VMEM((Z, Q, 128), f32),
-        pltpu.VMEM((CORES * G, Q, 128), f32),
-        pltpu.VMEM((Z, Q, 128), f32),
-        pltpu.VMEM((CORES * G, Q, 128), f32),
+        pltpu.VMEM((2, Z, Q // 2, 128), f32),
+        pltpu.VMEM((2, CORES * G, Q // 2, 128), f32),
+        pltpu.VMEM((2, Z, Q // 2, 128), f32),
+        pltpu.VMEM((2, CORES * G, Q // 2, 128), f32),
         pltpu.VMEM((Z, 8, 128), f32),
         pltpu.VMEM((CORES * G, -(-Z // 8) * 8, 128), f32),
         pltpu.VMEM((2, W + 2, 24, K), f32),
@@ -528,10 +529,10 @@
         dma((4, G)), dma((4, G)),
         dma((6,)), dma((6,)),
         dma((2,)), dma((2,)),
-        dma((Z,)), dma((Z,)),
-        dma((CORES * G,)), dma((CORES * G,)),
-        dma((Z,)), dma((Z,)),
-        dma((CORES * G,)), dma((CORES * G,)),
+        dma((2, Z)), dma((2, Z)),
+        dma((2, CORES * G)), dma((2, CORES * G)),
+        dma((2, Z)), dma((2, Z)),
+        dma((2, CORES * G)), dma((2, CORES * G)),
         dma((Z,)), dma((Z,)),
         dma((CORES * G,)), dma((CORES * G,)),
     ]

time: 26.5 us -> 28.8 us (1.087)
  Pallas kernels: 25.7 us -> 28 us
    pallas_call x1, Pallas kernels: 25 us -> 27.3 us  [body(): pl.pallas_call(functools.partial(kernel, G, C), out_shape=(pltpu.VMEM((2,...]
where the time goes in v3:
time: 28.8 us; the launch traced here: 28.6 us
  Pallas kernels  28 us (97%)
  between operations  0.64 us (2%)
    pallas_call x1, Pallas kernels, body(): pl.pallas_call(functools.partial(kernel, G, C), out_shape=(pltpu.VMEM((2,...  27.3 us
    pallas_call x1, Pallas kernels, body(): pl.pallas_call(deliver, out_shape=tuple((jax.ShapeDtypeStruct(x.shape, x....  0.67 us

profile of v3, /device:TPU:0, one launch (start us, length us, event | category | flops | bytes accessed | tf_op | source)
XLA Modules:
  0.0 28.6 jit_solution(5285972849619369663)
XLA Ops:
  0.6 27.3 %shard_map.102 = (f32[2,8,4,128]{3,2,1,0:T(4,128)S(1)}, f32[2,8,4,128]{3,2,1,0:T(4,128)S(1)}, f32[2,256]{1,0:T(2,128)S(1)}, f32[1,8]{1,0:T(1,128)S(1)}) custom-call(f32[8,4,128]{2,1,0:T(4,128)} %den_in.1, f32[8,4,128]{2,1,0:T(4,128)} %sus_in.1, s32[2,256]{1,0:T(2,128)} %cell_in.1, s32[2,256]{1,0:T(2,128)} %line_in.1, f32[2,256]{1,0:T(2,128)} %obs_in.1, ...), custom_call_target="tpu_custom_call" | custom-call | tf_op jit(solution)/shard_map/pallas_call | solution.py:539
  27.9 0.7 %shard_map.103 = (f32[2,8,4,128]{3,2,1,0:T(4,128)}, f32[2,8,4,128]{3,2,1,0:T(4,128)}, f32[2,256]{1,0:T(2,128)}, f32[1,8]{1,0:T(1,128)}) custom-call(f32[2,8,4,128]{3,2,1,0:T(4,128)S(1)} %get-tuple-element.12.refs_0_, f32[2,8,4,128]{3,2,1,0:T(4,128)S(1)} %get-tuple-element.13.refs_1_, f32[2,256]{1,0:T(2,128)S(1)} %get-tuple-element.14.refs_2_, ...), custom_call_target="tpu_custom_call" | custom-call | tf_op jit(solution)/shard_map/pallas_call | solution.py:554

commit v4 on v2

--- a/solution.py
+++ b/solution.py
@@ -63,7 +63,7 @@
 def kernel(
     G, C, den_in, sus_in, cell_in, line_in, obs_in, wgt_in, steps_in,
     dg_out, cf_out, wr_out, tv_out,
-    den, sus, steps, s_in, E2, RS, F, A, cellb, lineb, obsb, wgtb, OY, OX, OHI, OLO, wrs,
+    den, sus, steps, s_in, E2, RS, F, A, st, cellb, lineb, obsb, wgtb, OY, OX, OHI, OLO, wrs,
     b1, b2, c1, c2, s1, s2, M, SH, RH, CH, CR, CFX, GE,
     s_st, r_st, s_h, r_h, s_c, r_c, s_b1, r_b1, s_b2, r_b2, s_c1, r_c1, s_c2, r_c2, s_s1, r_s1, s_s2, r_s2,
 ):
@@ -120,10 +120,10 @@
             (
                 (den_in, den),
                 (sus_in, sus),
-                (cell_in, cellb.at[mx]),
-                (line_in, lineb.at[mx]),
-                (obs_in, obsb.at[mx]),
-                (wgt_in, wgtb.at[mx]),
+                (cell_in, cellb),
+                (line_in, lineb),
+                (obs_in, obsb),
+                (wgt_in, wgtb),
                 (steps_in, steps),
             )
         )
@@ -182,6 +182,34 @@
     own_columns = [[models[f][:, j, :] for j in range(W)] for f in range(2)]
     b1[chip] = forward(own_columns[0], 0) + forward(own_columns[1], 1)
 
+    pl.semaphore_wait(barrier, len(partners))
+
+    def copy(src, dst, ssem, rsem, where):
+        return pltpu.make_async_remote_copy(
+            src_ref=src, dst_ref=dst, send_sem=ssem, recv_sem=rsem,
+            device_id=where, device_id_type=MESH,
+        )
+
+    pending = []
+
+    def share(buf, ssem, rsem, group):
+        targets, mine, _ = groups[group]
+        for d, where in enumerate(targets):
+            one = copy(buf.at[mine], buf.at[mine], ssem.at[d], rsem.at[mine], where)
+            one.start()
+            pending.append(one)
+
+    def arrived(buf, ssem, rsem, group):
+        targets, _, sources = groups[group]
+        for src in sources:
+            copy(buf.at[src], buf.at[src], ssem.at[0], rsem.at[src], targets[0]).wait_recv()
+
+    share(b1, s_b1, r_b1, "z")
+    for one in loads[2:]:
+        one.wait()
+    for n, buf in enumerate((cellb, lineb, obsb, wgtb)):
+        st[mx, 2 * n : 2 * n + 2, :] = buf[...].astype(f32)
+    share(st, s_st, r_st, "x")
     M[...] = jnp.zeros(M.shape, f32)
     F[...] = jnp.zeros(F.shape, f32)
     A[...] = jnp.zeros(A.shape, f32)
@@ -198,35 +226,6 @@
         SH[3, f, 0:R, :] = own_columns[f][0]
         SH[4, f, 0:1, :] = models[f][R - 1, 0:1, :]
         SH[5, f, 0:1, :] = models[f][0, W - 1 : W, :]
-    for one in loads[2:]:
-        one.wait()
-
-    pl.semaphore_wait(barrier, len(partners))
-
-    def copy(src, dst, ssem, rsem, where):
-        return pltpu.make_async_remote_copy(
-            src_ref=src, dst_ref=dst, send_sem=ssem, recv_sem=rsem,
-            device_id=where, device_id_type=MESH,
-        )
-
-    pending = []
-
-    def share(buf, ssem, rsem, group):
-        targets, mine, _ = groups[group]
-        for d, where in enumerate(targets):
-            one = copy(buf.at[mine], buf.at[mine], ssem.at[d], rsem.at[mine], where)
-            one.start()
-            pending.append(one)
-
-    def arrived(buf, ssem, rsem, group):
-        targets, _, sources = groups[group]
-        for src in sources:
-            copy(buf.at[src], buf.at[src], ssem.at[0], rsem.at[src], targets[0]).wait_recv()
-
-    share(b1, s_b1, r_b1, "z")
-    station_bufs = (cellb, lineb, obsb, wgtb)
-    for n, buf in enumerate(station_bufs):
-        share(buf, s_st.at[n], r_st.at[n], "x")
     halo_targets = [at(1, 0), at(-1, 0), at(0, 1), at(0, -1), at(1, -1), at(-1, 1)]
     halos = []
     for n, where in enumerate(halo_targets):
@@ -235,17 +234,25 @@
         halos.append(one)
         pending.append(one)
 
-    for n, buf in enumerate(station_bufs):
-        arrived(buf, s_st.at[n], r_st.at[n], "x")
-
-    def spread_out(buf):
-        return jnp.concatenate([buf[g, f : f + 1, :] for g in range(G) for f in range(2)], axis=1)
+    arrived(b1, s_b1, r_b1, "z")
+    partial = b1[0]
+    for n in range(1, Z):
+        partial = partial + b1[n]
+    b2[slot] = partial
+    share(b2, s_b2, r_b2, "g")
+
+    arrived(st, s_st, r_st, "x")
+
+    def spread_out(n):
+        return jnp.concatenate(
+            [st[g, 2 * n + f : 2 * n + f + 1, :] for g in range(G) for f in range(2)], axis=1
+        )
 
     field_of = (iota((1, ST), 1) // own) % 2
-    cells = spread_out(cellb)
-    lines = spread_out(lineb)
-    observed = spread_out(obsb)
-    weight = spread_out(wgtb)
+    cells = spread_out(0).astype(jnp.int32)
+    lines = spread_out(1).astype(jnp.int32)
+    observed = spread_out(2)
+    weight = spread_out(3)
     at_x = cells // NY
     at_y = cells - at_x * NY
     key_lane = (at_x % xp) * V + field_of * NY + at_y
@@ -271,13 +278,6 @@
         parts = jnp.concatenate(split3(grid), axis=0)
         back = lax.dot_general(parts, OY[...], NN, preferred_element_type=f32)
         return jnp.sum(thirds(back) * OX[...], axis=0, keepdims=True)
-
-    arrived(b1, s_b1, r_b1, "z")
-    partial = b1[0]
-    for n in range(1, Z):
-        partial = partial + b1[n]
-    b2[slot] = partial
-    share(b2, s_b2, r_b2, "g")
 
     for one in halos:
         one.wait_recv()
@@ -503,10 +503,11 @@
         pltpu.VMEM((2, 2 * (W + 1) * 16, N), bf16),
         pltpu.VMEM((2, W + 1, 2, NX + 24, 128), f32),
         pltpu.VMEM((2, Q + 16, 128), f32),
-        pltpu.VMEM((G, 2, own), jnp.int32),
-        pltpu.VMEM((G, 2, own), jnp.int32),
-        pltpu.VMEM((G, 2, own), f32),
-        pltpu.VMEM((G, 2, own), f32),
+        pltpu.VMEM((G, 8, own), f32),
+        pltpu.VMEM((2, own), jnp.int32),
+        pltpu.VMEM((2, own), jnp.int32),
+        pltpu.VMEM((2, own), f32),
+        pltpu.VMEM((2, own), f32),
         pltpu.VMEM((128, ST), bf16),
         pltpu.VMEM((Q, ST), f32),
         pltpu.VMEM((2 * HIGH, ST), f32),
@@ -525,7 +526,7 @@
         pltpu.VMEM((2, 2, 8, K), f32),
         pltpu.VMEM((2, W + 1, 16, K), f32),
         pltpu.VMEM((2, W + 1, 24, K), f32),
-        dma((4, G)), dma((4, G)),
+        dma((G,)), dma((G,)),
         dma((6,)), dma((6,)),
         dma((2,)), dma((2,)),
         dma((Z,)), dma((Z,)),

time: 26.5 us -> 25.9 us (0.977)
  Pallas kernels: 25.7 us -> 25.1 us
    pallas_call x1, Pallas kernels: 25 us -> 24.4 us  [body(): pl.pallas_call(functools.partial(kernel, G, C), out_shape=(pltpu.VMEM((2,...]
where the time goes in v4:
time: 25.9 us; the launch traced here: 25.7 us
  Pallas kernels  25.1 us (97%)
  between operations  0.64 us (2%)
    pallas_call x1, Pallas kernels, body(): pl.pallas_call(functools.partial(kernel, G, C), out_shape=(pltpu.VMEM((2,...  24.4 us
    pallas_call x1, Pallas kernels, body(): pl.pallas_call(deliver, out_shape=tuple((jax.ShapeDtypeStruct(x.shape, x....  0.67 us

profile of v4, /device:TPU:0, one launch (start us, length us, event | category | flops | bytes accessed | tf_op | source)
XLA Modules:
  0.0 25.7 jit_solution(15016177349712359178)
XLA Ops:
  0.6 24.4 %shard_map.102 = (f32[2,8,4,128]{3,2,1,0:T(4,128)S(1)}, f32[2,8,4,128]{3,2,1,0:T(4,128)S(1)}, f32[2,256]{1,0:T(2,128)S(1)}, f32[1,8]{1,0:T(1,128)S(1)}) custom-call(f32[8,4,128]{2,1,0:T(4,128)} %den_in.1, f32[8,4,128]{2,1,0:T(4,128)} %sus_in.1, s32[2,256]{1,0:T(2,128)} %cell_in.1, s32[2,256]{1,0:T(2,128)} %line_in.1, f32[2,256]{1,0:T(2,128)} %obs_in.1, ...), custom_call_target="tpu_custom_call" | custom-call | tf_op jit(solution)/shard_map/pallas_call | solution.py:539
  25.0 0.7 %shard_map.103 = (f32[2,8,4,128]{3,2,1,0:T(4,128)}, f32[2,8,4,128]{3,2,1,0:T(4,128)}, f32[2,256]{1,0:T(2,128)}, f32[1,8]{1,0:T(1,128)}) custom-call(f32[2,8,4,128]{3,2,1,0:T(4,128)S(1)} %get-tuple-element.12.refs_0_, f32[2,8,4,128]{3,2,1,0:T(4,128)S(1)} %get-tuple-element.13.refs_1_, f32[2,256]{1,0:T(2,128)S(1)} %get-tuple-element.14.refs_2_, ...), custom_call_target="tpu_custom_call" | custom-call | tf_op jit(solution)/shard_map/pallas_call | solution.py:554
